TPU v7x, 256 devices: a whole 4x4x8 slice. The times are simulated.
256 devices in a mesh: fac: 32 (over y, z), cust: 8 (over x, core).
Axes of the slice: x: 4, y: 4, z: 8, core: 2. Of those that a mesh axis runs over, the one named last changes fastest.
Arguments:
- fac_coords: bfloat16 [16384, 128], P('fac'), may hold values from -6 to 6
- cust_coords: bfloat16 [131072, 128], P(('cust', 'fac')), may hold values from -6 to 6
- open_flags: int32 [16384], P('fac'), may hold values 0 or 1
- demand: int32 [131072], P('cust'), may hold values from 1 to 4
- fixed_cost: float32 [16384], P('fac'), may hold values from 0 to 64
- capacity: float32 [16384], P('fac'), may hold values from 16 to 64
- cap_mult: float32 [16384], P('fac'), may hold values from 0 to 0.1
- cover_mult: float32 [131072], P('cust'), may hold values from 0 to 2, as said below
Outputs:
- cover_final: float32 [131072], P('cust')
- cap_final: float32 [16384], P('fac')
- bounds: float32 [3], replicated
Inputs may be any that keep to these rules, and one draw needn't show every extreme that they name: `cover_mult`: initial coverage multipliers, all in one band of width 0.4.
All inputs are finite; a program needn't handle non-finite values. No bound on the sum of `open_flags` on one device may be relied on, other than what follows from the above.
Results may differ from a plain program's by a relative error of at most 0.0003.
Values may be sent and summed in bfloat16 or wider, within the bound.
A program may use at most 64 MiB of HBM per device.

v0:
```python
import functools
import math

import jax
import jax.numpy as jnp
from jax import lax
from jax.experimental import pallas as pl
from jax.experimental.pallas import tpu as pltpu
from jax.sharding import PartitionSpec as P

MESH = pl.DeviceIdType.MESH
ITERS = 3
TAU = 0.1
ALIGN = 16
ROWS = 256
F32 = jnp.float32
BF16 = jnp.bfloat16
VMEM = pl.BlockSpec(memory_space=pltpu.VMEM)


def split3(v):
    a = v.astype(BF16)
    r = v - a.astype(F32)
    b = r.astype(BF16)
    c = (r - b.astype(F32)).astype(BF16)
    return a, b, c


def onehot_of(open_row):
    n = open_row.shape[1]
    flags = jnp.broadcast_to(open_row.astype(F32), (16, n)).astype(BF16)
    tri = (lax.broadcasted_iota(jnp.int32, (n, n), 0) <= lax.broadcasted_iota(jnp.int32, (n, n), 1)).astype(F32).astype(BF16)
    pos = jnp.dot(flags, tri, preferred_element_type=F32)[0:1]
    pos = jnp.where(open_row > 0, pos - 1.0, -1.0).astype(jnp.int32)
    hit = lax.broadcasted_iota(jnp.int32, (n, n), 0) == pos
    return jnp.where(hit, 1.0, 0.0).astype(BF16)


def nt(a, b):
    return lax.dot_general(a, b, (((1,), (1,)), ((), ())), preferred_element_type=F32)


def pre_kernel(open_ref, fac_ref, cap_ref, mu_ref, fixed_ref, cust_ref, demand_ref, cover_ref,
               comp_ref, info_ref, cust_t_ref, hq_ref, wt_ref, lam_ref, ext_ref, shut_ref):
    n, width = fac_ref.shape
    cols = cust_ref.shape[0]
    nc, _, part = info_ref.shape
    f, c = lax.axis_index("fac"), lax.axis_index("cust")
    mine = pl.ds(pl.multiple_of(f * cols, cols), cols)
    wt_ref[...] = demand_ref[:, mine].astype(F32)
    lam_ref[...] = cover_ref[:, mine]
    opened = open_ref[...].astype(F32)
    shut = mu_ref[...]
    ext = jnp.zeros((8, 128), F32)
    lane = lax.broadcasted_iota(jnp.int32, (8, 128), 1)
    for k in range(ITERS):
        fixed = jnp.sum(opened * fixed_ref[...] - (1.0 - opened) * shut * cap_ref[...])
        ext = ext + jnp.where((lane == k) & (c == 0), fixed, 0.0)
        shut = jnp.maximum(0.0, shut - 0.1 / (k + 1))
    ext_ref[...] = ext
    shut_ref[...] = shut
    hot = onehot_of(open_ref[...])
    fac = fac_ref[...]
    comp_ref[...] = jnp.dot(hot, fac, preferred_element_type=F32).astype(BF16)
    sq = fac.astype(F32) ** 2
    s1, s2, _ = split3(sq)
    ones = jnp.ones((16, width), BF16)
    half = -0.5 * (nt(ones, s1) + nt(ones, s2))[0:1]
    rows = [jnp.ones((1, n), BF16)]
    for v in (half, mu_ref[...], cap_ref[...]):
        rows.extend(split3(v))
    rows = [r.astype(F32) for r in rows] + [jnp.zeros((6, n), F32)]
    got = nt(jnp.concatenate(rows, axis=0).astype(BF16), hot)
    rows = [got[0:1]] + [got[3 * m + 1:3 * m + 2] + got[3 * m + 2:3 * m + 3] + got[3 * m + 3:3 * m + 4] for m in range(3)]
    info = jnp.concatenate(rows + [jnp.zeros((4, n), F32)], axis=0)
    for p in range(nc):
        info_ref[p] = info[:, p * part:(p + 1) * part]
    eye = (lax.broadcasted_iota(jnp.int32, (width, width), 0) == lax.broadcasted_iota(jnp.int32, (width, width), 1)).astype(F32).astype(BF16)
    turned = nt(eye, cust_ref[...])
    cust_t_ref[...] = turned.astype(BF16)
    hq_ref[...] = 0.5 * jnp.sum(turned * turned, axis=0, keepdims=True)


def sync(peers):
    barrier = pltpu.get_barrier_semaphore()
    for peer in peers:
        pl.semaphore_signal(barrier, inc=1, device_id=peer, device_id_type=MESH)
    pl.semaphore_wait(barrier, len(peers))


def gather_kernel(nf, nc, comp_ref, info_ref, facs_ref, infos_ref, s1, r1, s2, r2, s3, r3, loc):
    f, c = lax.axis_index("fac"), lax.axis_index("cust")
    fp = [(lax.rem(f + d, nf), c) for d in range(1, nf)]
    half = nc // 2
    core = lax.rem(c, 2)
    twin = (f, c + 1 - 2 * core)
    sides = [lax.rem(c + 2 * d, nc) for d in range(1, half)]
    part = comp_ref.shape[0] // nc
    sync(fp + [(f, e) for e in sides] + [twin])

    def rows(q):
        return pl.ds(pl.multiple_of(q * part, part), part)

    def move(src, q, k, send, recv, peer, own=False):
        a = comp_ref.at[rows(q)] if own else facs_ref.at[src, rows(q)]
        b = info_ref.at[q] if own else infos_ref.at[src, q]
        pair = [
            pltpu.make_async_remote_copy(a, facs_ref.at[src, rows(q)], send.at[k, 0], recv.at[k, 0], device_id=peer, device_id_type=MESH),
            pltpu.make_async_remote_copy(b, infos_ref.at[src, q], send.at[k, 1], recv.at[k, 1], device_id=peer, device_id_type=MESH),
        ]
        for cpy in pair:
            cpy.start()
        return pair

    first = [move(f, c, d, s1, r1, peer, True) for d, peer in enumerate(fp)]
    own = pltpu.make_async_copy(comp_ref, facs_ref.at[f], loc.at[0])
    own.start()
    own_info = pltpu.make_async_copy(info_ref, infos_ref.at[f], loc.at[1])
    own_info.start()
    across, over = [], []
    for d in range(nf - 1):
        src = lax.rem(f + nf - 1 - d, nf)
        for cpy in first[d]:
            cpy.wait_recv()
        for e, q in enumerate(sides):
            across.append((src, lax.rem(c + nc - 2 * (e + 1), nc), move(src, c, d * (half - 1) + e, s2, r2, (f, q))))
        over.append(move(src, c, d * half, s3, r3, twin))
        for e in range(half - 1):
            if d > 0:
                ready = across[(d - 1) * (half - 1) + e]
                for cpy in ready[2]:
                    cpy.wait_recv()
                over.append(move(ready[0], ready[1], (d - 1) * half + 1 + e, s3, r3, twin))
    for e in range(half - 1):
        ready = across[(nf - 2) * (half - 1) + e]
        for cpy in ready[2]:
            cpy.wait_recv()
        over.append(move(ready[0], ready[1], (nf - 2) * half + 1 + e, s3, r3, twin))
    for pair in first + [a[2] for a in across]:
        for cpy in pair:
            cpy.wait_send()
    for pair in over:
        for cpy in pair:
            cpy.wait()
    own.wait()
    own_info.wait()


def step_kernel(step, facs_ref, infos_ref, mu_ref, load_ref, cust_t_ref, hq_ref, lam_ref, wt_ref, ext_ref,
                part_ref, mu_out_ref, lam_out_ref, tot_ref,
                info_ref, a_ref, w_ref, y_ref, x_ref, d_ref, acc_ref, cov_ref, soft_ref):
    first, size, prev = step == 0, 0.1 / (step + 1), 0.1 / max(step, 1)
    nf, n, width = facs_ref.shape
    cols = cust_t_ref.shape[1]
    block = y_ref.shape[2]
    tiles = cols // block
    lam = lam_ref[...]
    wt = wt_ref[...]
    a1, a2, a3 = split3(64.0 * lam - hq_ref[...])
    one_c = jnp.ones((3, cols), F32)
    mw = jnp.broadcast_to(-64.0 * wt, (3, cols))
    aug = jnp.concatenate([a1.astype(F32), a2.astype(F32), a3.astype(F32), one_c, mw, jnp.zeros((7, cols), F32)], axis=0)
    w_ref[0:width, :] = cust_t_ref[...]
    w_ref[width:width + 16, :] = aug.astype(BF16)
    w_ref[width + 16:, :] = jnp.zeros((width - 16, cols), BF16)
    cov_ref[...] = jnp.zeros_like(cov_ref)
    soft_ref[...] = jnp.zeros_like(soft_ref)
    lane = lax.broadcasted_iota(jnp.int32, (ROWS, width), 1)
    pad = jnp.where(lane == 3, -30000.0, 0.0).astype(BF16)
    sel = (lax.broadcasted_iota(jnp.int32, (16, width), 0) == lax.broadcasted_iota(jnp.int32, (16, width), 1)).astype(F32).astype(BF16)
    top = (lax.broadcasted_iota(jnp.int32, (16, 128), 0) == 0).astype(F32).astype(BF16)
    wrows = jnp.concatenate([wt, jnp.zeros((15, cols), F32)], axis=0).astype(BF16)
    d_ref[...] = lax.dot_general(wrows, top, (((0,), (0,)), ((), ())), preferred_element_type=F32).astype(BF16)
    nc, part = infos_ref.shape[1], infos_ref.shape[3]
    for f in range(nf):
        info_ref[f] = jnp.concatenate([infos_ref[f, p] for p in range(nc)], axis=1)
    offs = []
    off = jnp.int32(0)
    one_r = jnp.ones((3, n), F32)
    for f in range(nf):
        valid = info_ref[f, 0:1, :]
        cap = info_ref[f, 3:4, :]
        if first:
            mu = info_ref[f, 2:3, :]
        else:
            mu = mu_ref[f:f + 1, :]
            load = load_ref[f:f + 1, :]
            mu = jnp.maximum(0.0, mu + prev * (load - cap) / (load + jnp.where(valid > 0, cap, 1.0)))
        mu = mu * valid
        mu_out_ref[f:f + 1, :] = mu
        b = jnp.where(valid > 0, info_ref[f, 1:2, :], -30000.0)
        parts = [p.astype(F32) for p in split3(b) + split3(mu)]
        rows = jnp.concatenate([one_r] + parts + [jnp.zeros((7, n), F32)], axis=0).astype(BF16)
        side = lax.dot_general(rows, sel, (((0,), (0,)), ((), ())), preferred_element_type=F32).astype(BF16)
        count = jnp.sum(valid).astype(jnp.int32)
        off = pl.multiple_of(off, ALIGN)
        offs.append(off)
        a_ref[pl.ds(off, n), 0:width] = facs_ref[f]
        a_ref[pl.ds(off, n), width:2 * width] = side
        off = off + ((count + ALIGN - 1) // ALIGN) * ALIGN
    tail = pl.multiple_of(off, ALIGN)
    a_ref[pl.ds(tail, ROWS), 0:width] = jnp.zeros((ROWS, width), BF16)
    a_ref[pl.ds(tail, ROWS), width:2 * width] = pad
    n_blocks = (off + ROWS - 1) // ROWS
    scale = math.log2(math.e) / 6.4

    def body(i, _):
        base = pl.multiple_of(i * ROWS, ROWS)
        lhs = a_ref[pl.ds(base, ROWS), :]

        def dot(t):
            y_ref[t % 2] = jnp.dot(lhs, w_ref[:, t * block:(t + 1) * block], preferred_element_type=F32)

        dot(0)
        for t in range(tiles):
            if t + 1 < tiles:
                dot(t + 1)
            covs = [cov_ref[:, t * block + q * 128:t * block + (q + 1) * 128] for q in range(block // 128)]
            softs = [soft_ref[:, t * block + q * 128:t * block + (q + 1) * 128] for q in range(block // 128)]
            for r in range(0, ROWS, 32):
                for q in range(block // 128):
                    es = [jnp.exp2(y_ref[t % 2, r + 8 * s:r + 8 * s + 8, q * 128:(q + 1) * 128] * scale) for s in range(4)]
                    us = [1.0 + e for e in es]
                    p01 = us[0] * us[1]
                    p23 = us[2] * us[3]
                    r01 = 1.0 / p01
                    r23 = 1.0 / p23
                    xs = [es[0] * (us[1] * r01), es[1] * (us[0] * r01), es[2] * (us[3] * r23), es[3] * (us[2] * r23)]
                    covs[q] = covs[q] + ((xs[0] + xs[1]) + (xs[2] + xs[3]))
                    softs[q] = softs[q] + jnp.log(p01 * p23)
                    for h in range(2):
                        both = jnp.concatenate([xs[2 * h], xs[2 * h + 1]], axis=0).astype(BF16)
                        x_ref[t % 2, r + 16 * h:r + 16 * h + 16, q * 128:(q + 1) * 128] = both
            got = jnp.dot(x_ref[t % 2], d_ref[t * block:(t + 1) * block, :], preferred_element_type=F32)
            at = pl.ds(base, ROWS)
            acc_ref[at, :] = got if t == 0 else acc_ref[at, :] + got
            for q in range(block // 128):
                cov_ref[:, t * block + q * 128:t * block + (q + 1) * 128] = covs[q]
                soft_ref[:, t * block + q * 128:t * block + (q + 1) * 128] = softs[q]
        return 0

    lax.fori_loop(0, n_blocks, body, 0)
    diag = lax.broadcasted_iota(jnp.int32, (128, 128), 0) == lax.broadcasted_iota(jnp.int32, (128, 128), 1)
    for f in range(nf):
        for b in range(n // 128):
            at = pl.ds(pl.multiple_of(offs[f] + b * 128, ALIGN), 128)
            got = jnp.sum(jnp.where(diag, acc_ref[at, :], 0.0), axis=0, keepdims=True)
            part_ref[f:f + 1, b * 128:(b + 1) * 128] = jnp.where(info_ref[f, 0:1, b * 128:(b + 1) * 128] > 0, got, 0.0)
    cover = jnp.sum(cov_ref[...], axis=0, keepdims=True)
    soft = jnp.sum(soft_ref[...], axis=0, keepdims=True)
    me, c = lax.axis_index("fac"), lax.axis_index("cust")
    mine = jnp.sum(mu_out_ref[pl.ds(me, 1), :] * info_ref[me, 3:4, :])
    here = jnp.sum(wt * lam - TAU * wt * soft) - jnp.where(c == 0, mine, 0.0)
    spot = lax.broadcasted_iota(jnp.int32, (8, 128), 1) == step
    tot = ext_ref[...] + jnp.where(spot, here, 0.0)
    tot_ref[...] = tot
    if part_ref.shape[0] > nf:
        part_ref[nf:nf + 8, :] = jnp.zeros((8, n), F32)
        part_ref[nf:nf + 8, 0:128] = tot
    lam_out_ref[...] = lam + size * wt * (1.0 - cover) / (1.0 + cover)


def exchange(peers, src, slots, send, recv):
    copies = []
    for d, peer in enumerate(peers):
        cpy = pltpu.make_async_remote_copy(src, slots.at[d], send.at[d], recv.at[d], device_id=peer, device_id_type=MESH)
        cpy.start()
        copies.append(cpy)
    return copies


def reduce_kernel(nf, nc, x_ref, lam_ref, out_ref, lam_out, got1, mid, got2, s1, r1, s2, r2, s3, r3, loc):
    f, c = lax.axis_index("fac"), lax.axis_index("cust")
    fp = [(lax.rem(f + d, nf), c) for d in range(1, nf)]
    cp = [(f, lax.rem(c + d, nc)) for d in range(1, nc)]
    sync(fp + cp)
    first = exchange(cp, x_ref, got1, s1, r1)
    lams = []
    if lam_ref is not None:
        own = pltpu.make_async_copy(lam_ref, lam_out.at[f], loc)
        own.start()
        for d, peer in enumerate(fp):
            cpy = pltpu.make_async_remote_copy(lam_ref, lam_out.at[f], s3.at[d], r3.at[d], device_id=peer, device_id_type=MESH)
            cpy.start()
            lams.append(cpy)
    total = x_ref[...]
    for d, cpy in enumerate(first):
        cpy.wait()
        total = total + got1[d]
    mid[...] = total
    second = exchange(fp, mid, got2, s2, r2)
    for d, cpy in enumerate(second):
        cpy.wait()
        total = total + got2[d]
    out_ref[...] = total
    for cpy in lams:
        cpy.wait()
    if lam_ref is not None:
        own.wait()


def reduce_plain(nf, nc, x_ref, out_ref, got1, mid, got2, s1, r1, s2, r2):
    reduce_kernel(nf, nc, x_ref, None, out_ref, None, got1, mid, got2, s1, r1, s2, r2, None, None, None)


def finish_kernel(total_cust, total_ref, mu_ref, infos_ref, open_ref, shut_ref, out_ref, bound_ref):
    nf, nc = infos_ref.shape[0:2]
    n = open_ref.shape[1]
    f = lax.axis_index("fac")
    load = total_ref[pl.ds(f, 1), :]
    cap = jnp.concatenate([infos_ref[f, p, 3:4, :] for p in range(nc)], axis=1)
    new = jnp.maximum(0.0, mu_ref[pl.ds(f, 1), :] + (0.1 / ITERS) * (load - cap) / (load + jnp.where(cap > 0, cap, 1.0)))
    rows = jnp.concatenate([v.astype(F32) for v in split3(new)] + [jnp.zeros((13, n), F32)], axis=0).astype(BF16)
    got = jnp.dot(rows, onehot_of(open_ref[...]), preferred_element_type=F32)
    out_ref[...] = jnp.where(open_ref[...] > 0, got[0:1] + got[1:2] + got[2:3], shut_ref[...])
    bound_ref[...] = total_ref[nf:nf + 1, 0:128] / total_cust


def params(cid=None, mib=56):
    return pltpu.CompilerParams(collective_id=cid, has_side_effects=True, vmem_limit_bytes=mib * 2 ** 20) if cid is not None else pltpu.CompilerParams(vmem_limit_bytes=mib * 2 ** 20)


def local(nf, nc, fac_coords, cust_coords, open_flags, demand, fixed_cost, capacity, cap_mult, cover_mult):
    n, width = fac_coords.shape
    cols = cust_coords.shape[0]
    total_cust = cols * nf * nc
    sd = jax.ShapeDtypeStruct
    dma = pltpu.SemaphoreType.DMA
    part = n // nc
    open_row = open_flags.reshape(1, n)
    comp, info, cust_t, hq, wt, lam, ext, shut = pl.pallas_call(
        pre_kernel,
        out_shape=(sd((n, width), BF16), sd((nc, 8, part), F32), sd((width, cols), BF16), sd((1, cols), F32),
                   sd((1, cols), F32), sd((1, cols), F32), sd((8, 128), F32), sd((1, n), F32)),
        in_specs=[VMEM] * 8, out_specs=(VMEM,) * 8, compiler_params=params(), name="pre",
    )(open_row, fac_coords, capacity.reshape(1, n), cap_mult.reshape(1, n), fixed_cost.reshape(1, n), cust_coords,
      demand.reshape(1, nf * cols), cover_mult.reshape(1, nf * cols))
    sides = (nf - 1) * (nc // 2 - 1)
    facs, infos = pl.pallas_call(
        functools.partial(gather_kernel, nf, nc),
        out_shape=(sd((nf, n, width), BF16), sd((nf, nc, 8, part), F32)),
        in_specs=[VMEM] * 2, out_specs=(VMEM,) * 2,
        scratch_shapes=[dma((nf - 1, 2)), dma((nf - 1, 2)), dma((sides, 2)), dma((sides, 2)),
                        dma(((nf - 1) * (nc // 2), 2)), dma(((nf - 1) * (nc // 2), 2)), dma((2,))],
        compiler_params=params(0), name="gather",
    )(comp, info)
    block = math.gcd(cols, 512)
    total_rows = nf * n
    mu = load = hq
    tot = ext
    for step in range(ITERS):
        last = step == ITERS - 1
        rows = nf + 8 if last else nf
        payload, mu, lam, tot = pl.pallas_call(
            functools.partial(step_kernel, step),
            out_shape=(sd((rows, n), F32), sd((nf, n), F32), sd((1, cols), F32), sd((8, 128), F32)),
            in_specs=[VMEM] * 9, out_specs=(VMEM,) * 4,
            scratch_shapes=[
                pltpu.VMEM((nf, 8, n), F32),
                pltpu.VMEM((total_rows + n + ROWS, 2 * width), BF16),
                pltpu.VMEM((2 * width, cols), BF16),
                pltpu.VMEM((2, ROWS, block), F32),
                pltpu.VMEM((2, ROWS, block), BF16),
                pltpu.VMEM((cols, 128), BF16),
                pltpu.VMEM((total_rows + n + ROWS, 128), F32),
                pltpu.VMEM((8, cols), F32),
                pltpu.VMEM((8, cols), F32),
            ],
            compiler_params=params(), name="step",
        )(facs, infos, mu, load, cust_t, hq, lam, wt, tot)
        scratch = [pltpu.VMEM((nc - 1, rows, n), F32), pltpu.VMEM((rows, n), F32), pltpu.VMEM((nf - 1, rows, n), F32),
                   dma((nc - 1,)), dma((nc - 1,)), dma((nf - 1,)), dma((nf - 1,))]
        if not last:
            load = pl.pallas_call(
                functools.partial(reduce_plain, nf, nc),
                out_shape=sd((rows, n), F32), in_specs=[VMEM], out_specs=VMEM,
                scratch_shapes=scratch, compiler_params=params(1 + step), name="reduce",
            )(payload)
        else:
            load, lam_all = pl.pallas_call(
                functools.partial(reduce_kernel, nf, nc),
                out_shape=(sd((rows, n), F32), sd((nf, 1, cols), F32)), in_specs=[VMEM] * 2, out_specs=(VMEM,) * 2,
                scratch_shapes=scratch + [dma((nf - 1,)), dma((nf - 1,)), dma(())],
                compiler_params=params(1 + step), name="reduce",
            )(payload, lam)
    cap_final, bounds = pl.pallas_call(
        functools.partial(finish_kernel, total_cust), out_shape=(sd((1, n), F32), sd((1, 128), F32)),
        in_specs=[VMEM] * 5, out_specs=(VMEM,) * 2, compiler_params=params(), name="finish",
    )(load, mu, infos, open_row, shut)
    return lam_all.reshape(nf * cols), cap_final.reshape(n), bounds[0, :ITERS]


def solution(mesh):
    nf, nc = mesh.shape["fac"], mesh.shape["cust"]
    return jax.shard_map(
        functools.partial(local, nf, nc),
        mesh=mesh,
        in_specs=(P("fac", None), P(("cust", "fac"), None), P("fac"), P("cust"), P("fac"), P("fac"), P("fac"), P("cust")),
        out_specs=(P("cust"), P("fac"), P()),
        check_vma=False,
    )
```

profile of v0, /device:TPU:1, one launch (start us, length us, event | category | flops | bytes accessed | tf_op | source)
XLA Modules:
  0.0 382.8 jit_solution(18418943855255454196)
XLA Ops:
  0.6 2.5 pre.1
  3.1 90.6 %gather.1 = (bf16[32,512,128]{2,1,0:T(8,128)(2,1)}, f32[32,8,8,64]{3,2,1,0:T(8,128)}) custom-call(bf16[512,128]{1,0:T(8,128)(2,1)} %get-tuple-element.28.comp_ref, f32[8,8,64]{2,1,0:T(8,128)} %get-tuple-element.29.info_ref), custom_call_target="tpu_custom_call" | custom-call | tf_op jit(solution)/shard_map/gather/pallas_call | solution.py:339
  93.7 24.4 %step.3 = (f32[32,512]{1,0:T(8,128)}, f32[32,512]{1,0:T(8,128)}, f32[1,512]{1,0:T(1,128)}, f32[8,128]{1,0:T(8,128)}) custom-call(bf16[32,512,128]{2,1,0:T(8,128)(2,1)} %get-tuple-element.30.facs_ref, f32[32,8,8,64]{3,2,1,0:T(8,128)} %get-tuple-element.31.infos_ref, f32[1,512]{1,0:T(1,128)} %get-tuple-element.32.mu_ref.load_ref.hq_ref, ...), custom_call_target="tpu_custom_call" | custom-call | tf_op jit(solution)/shard_map/step/pallas_call | solution.py:354
  118.1 63.5 %reduce.3.load_ref = f32[32,512]{1,0:T(8,128)} custom-call(f32[32,512]{1,0:T(8,128)} %get-tuple-element.38.x_ref), custom_call_target="tpu_custom_call" | custom-call | tf_op jit(solution)/shard_map/reduce/pallas_call | solution.py:374
  181.7 24.3 %step.4 = (f32[32,512]{1,0:T(8,128)}, f32[32,512]{1,0:T(8,128)}, f32[1,512]{1,0:T(1,128)}, f32[8,128]{1,0:T(8,128)}) custom-call(bf16[32,512,128]{2,1,0:T(8,128)(2,1)} %get-tuple-element.30.facs_ref, f32[32,8,8,64]{3,2,1,0:T(8,128)} %get-tuple-element.31.infos_ref, f32[32,512]{1,0:T(8,128)} %get-tuple-element.37.mu_ref, f32[32,512]{1,0:T(8,128)} %reduce.3.load_ref, ...), custom_call_target="tpu_custom_call" | custom-call | tf_op jit(solution)/shard_map/step/pallas_call | solution.py:354
  205.9 66.0 %reduce.4.load_ref = f32[32,512]{1,0:T(8,128)} custom-call(f32[32,512]{1,0:T(8,128)} %get-tuple-element.42.x_ref), custom_call_target="tpu_custom_call" | custom-call | tf_op jit(solution)/shard_map/reduce/pallas_call | solution.py:374
  271.9 24.4 %step.5 = (f32[40,512]{1,0:T(8,128)}, f32[32,512]{1,0:T(8,128)}, f32[1,512]{1,0:T(1,128)}, f32[8,128]{1,0:T(8,128)}) custom-call(bf16[32,512,128]{2,1,0:T(8,128)(2,1)} %get-tuple-element.30.facs_ref, f32[32,8,8,64]{3,2,1,0:T(8,128)} %get-tuple-element.31.infos_ref, f32[32,512]{1,0:T(8,128)} %get-tuple-element.41.mu_ref, f32[32,512]{1,0:T(8,128)} %reduce.4.load_ref, ...), custom_call_target="tpu_custom_call" | custom-call | tf_op jit(solution)/shard_map/step/pallas_call | solution.py:354
  296.3 81.5 %reduce.5 = (f32[40,512]{1,0:T(8,128)}, f32[32,1,512]{2,1,0:T(1,128)}) custom-call(f32[40,512]{1,0:T(8,128)} %get-tuple-element.45.x_ref, f32[1,512]{1,0:T(1,128)} %get-tuple-element.46.lam_ref), custom_call_target="tpu_custom_call" | custom-call | tf_op jit(solution)/shard_map/reduce/pallas_call | solution.py:380
  377.9 2.3 finish.1
  380.2 1.2 slice_bitcast_fusion
  381.3 1.5 copy.12
where the time goes:
time: 385 us; the launch traced here: 383 us
  Pallas kernels  379 us (98%)
    pallas_call x2, Pallas kernels, local(): pl.pallas_call(functools.partial(reduce_plain, nf, nc), out_shape=sd((row...  130 us
    pallas_call x1, Pallas kernels, local(): pl.pallas_call(functools.partial(gather_kernel, nf, nc), out_shape=(sd((n...  90.6 us
    pallas_call x1, Pallas kernels, local(): pl.pallas_call(functools.partial(reduce_kernel, nf, nc), out_shape=(sd((r...  81.5 us
    pallas_call x3, Pallas kernels, local(): pl.pallas_call(functools.partial(step_kernel, step), out_shape=(sd((rows,...  73.1 us

commit v1 on v0

v1 whole, which is shorter than its diff:
```python
import functools
import math

import jax
import jax.numpy as jnp
from jax import lax
from jax.experimental import pallas as pl
from jax.experimental.pallas import tpu as pltpu
from jax.sharding import PartitionSpec as P

MESH = pl.DeviceIdType.MESH
ITERS = 3
TAU = 0.1
ALIGN = 16
ROWS = 128
BLOCK = 512
CHUNKS = 4
NZ = 8
F32 = jnp.float32
BF16 = jnp.bfloat16
VMEM = pl.BlockSpec(memory_space=pltpu.VMEM)
SMEM = pl.BlockSpec(memory_space=pltpu.SMEM)


def split3(v):
    a = v.astype(BF16)
    r = v - a.astype(F32)
    b = r.astype(BF16)
    c = (r - b.astype(F32)).astype(BF16)
    return a, b, c


def onehot_of(open_row):
    n = open_row.shape[1]
    flags = jnp.broadcast_to(open_row.astype(F32), (16, n)).astype(BF16)
    tri = (lax.broadcasted_iota(jnp.int32, (n, n), 0) <= lax.broadcasted_iota(jnp.int32, (n, n), 1)).astype(F32).astype(BF16)
    pos = jnp.dot(flags, tri, preferred_element_type=F32)[0:1]
    pos = jnp.where(open_row > 0, pos - 1.0, -1.0).astype(jnp.int32)
    hit = lax.broadcasted_iota(jnp.int32, (n, n), 0) == pos
    return jnp.where(hit, 1.0, 0.0).astype(BF16)


def nt(a, b):
    return lax.dot_general(a, b, (((1,), (1,)), ((), ())), preferred_element_type=F32)


def tn(a, b):
    return lax.dot_general(a, b, (((0,), (0,)), ((), ())), preferred_element_type=F32)


def spots():
    f, c = lax.axis_index("fac"), lax.axis_index("cust")
    return f // NZ, lax.rem(f, NZ), c


def pre_kernel(open_ref, fac_ref, cap_ref, mu_ref, fixed_ref, demand_ref, cover_ref,
               comp_ref, info_ref, wt_ref, lam_ref, ext_ref, shut_ref):
    n, width = fac_ref.shape
    nz, cols = wt_ref.shape
    y, z, c = spots()
    for r in range(nz):
        mine = pl.ds(pl.multiple_of((y * nz + r) * cols, cols), cols)
        wt_ref[r:r + 1, :] = demand_ref[:, mine].astype(F32)
        lam_ref[r:r + 1, :] = cover_ref[:, mine]
    opened = open_ref[...].astype(F32)
    shut = mu_ref[...]
    ext = jnp.zeros((8, 128), F32)
    lane = lax.broadcasted_iota(jnp.int32, (8, 128), 1)
    sub = lax.broadcasted_iota(jnp.int32, (8, 128), 0)
    for k in range(ITERS):
        fixed = jnp.sum(opened * fixed_ref[...] - (1.0 - opened) * shut * cap_ref[...])
        ext = ext + jnp.where((lane == k) & (sub == 0) & (c == 0), fixed, 0.0)
        shut = jnp.maximum(0.0, shut - 0.1 / (k + 1))
    ext_ref[...] = ext
    shut_ref[...] = shut
    hot = onehot_of(open_ref[...])
    fac = fac_ref[...]
    comp_ref[...] = jnp.dot(hot, fac, preferred_element_type=F32).astype(BF16)
    sq = fac.astype(F32) ** 2
    s1, s2, _ = split3(sq)
    ones = jnp.ones((16, width), BF16)
    half = -0.5 * (nt(ones, s1) + nt(ones, s2))[0:1]
    rows = [jnp.ones((1, n), BF16)]
    for v in (half, mu_ref[...], cap_ref[...]):
        rows.extend(split3(v))
    rows = [r.astype(F32) for r in rows] + [jnp.zeros((6, n), F32)]
    got = nt(jnp.concatenate(rows, axis=0).astype(BF16), hot)
    rows = [got[0:1]] + [got[3 * m + 1:3 * m + 2] + got[3 * m + 2:3 * m + 3] + got[3 * m + 3:3 * m + 4] for m in range(3)]
    info_ref[...] = jnp.concatenate(rows + [jnp.zeros((4, n), F32)], axis=0)


def sync(peers):
    barrier = pltpu.get_barrier_semaphore()
    for peer in peers:
        pl.semaphore_signal(barrier, inc=1, device_id=peer, device_id_type=MESH)
    pl.semaphore_wait(barrier, len(peers))


def remote(src, dst, send, recv, peer):
    cpy = pltpu.make_async_remote_copy(src, dst, send, recv, device_id=peer, device_id_type=MESH)
    cpy.start()
    return cpy


def gather_kernel(ny, cust_ref, comp_ref, info_ref, all_ref, facs_ref, infos_ref, sz, rz, sy, ry):
    y, z, c = spots()
    hops = NZ // 2
    zp = [(y * NZ + lax.rem(z + s, NZ), c) for s in (1, NZ - 1)]
    yp = [(lax.rem(y + d, ny) * NZ + z, c) for d in range(1, ny)]
    part = cust_ref.shape[0] // CHUNKS
    sync(zp + yp)

    def move(d, s, j):
        src = lax.rem(z + (NZ - s if d == 0 else s), NZ)
        at = pl.ds(j * part, part)
        a = cust_ref.at[at] if s == 0 else all_ref.at[src, at]
        return remote(a, all_ref.at[src, at], sz.at[d, s, j], rz.at[d, s, j], zp[d])

    def valid(d, s, j):
        return s < hops - 1 or (s == hops - 1 and (j < CHUNKS // 2) == (d == 0))

    ring = {}
    for j in range(CHUNKS):
        for d in range(2):
            if valid(d, 0, j):
                ring[d, 0, j] = move(d, 0, j)
    side = []
    for k, peer in enumerate(yp):
        side.append(remote(info_ref, infos_ref.at[y], sy.at[k, 0], ry.at[k, 0], peer))
        side.append(remote(comp_ref, facs_ref.at[y], sy.at[k, 1], ry.at[k, 1], peer))
    all_ref[z] = cust_ref[...]
    facs_ref[y] = comp_ref[...]
    infos_ref[y] = info_ref[...]
    for s in range(hops):
        for j in range(CHUNKS):
            for d in range(2):
                if valid(d, s, j):
                    ring[d, s, j].wait_recv()
                    if valid(d, s + 1, j):
                        ring[d, s + 1, j] = move(d, s + 1, j)
    for cpy in ring.values():
        cpy.wait_send()
    for cpy in side:
        cpy.wait()


def step_kernel(step, ny, refs):
    first = step == 0
    if first:
        (facs_ref, infos_ref, cust_ref, lam_ref, wt_ref, ext_ref,
         load_ref, cover_ref, tot_ref, mu_out_ref, coords_ref, turned_ref, hq_ref,
         a_ref, w_ref, y_ref, x_ref, d_ref, acc_ref, cov_ref, soft_ref) = refs
    else:
        (coords_ref, infos_ref, turned_ref, hq_ref, mu_ref, lam_ref, wt_ref, ext_ref,
         load_ref, cover_ref, tot_ref,
         a_ref, w_ref, y_ref, x_ref, d_ref, acc_ref, cov_ref, soft_ref) = refs
    n = infos_ref.shape[2]
    nz, cols = lam_ref.shape
    width = coords_ref.shape[1]
    total = nz * cols
    tiles = total // BLOCK
    me_y, me_z, c = spots()
    if first:
        eye = (lax.broadcasted_iota(jnp.int32, (width, width), 0) == lax.broadcasted_iota(jnp.int32, (width, width), 1)).astype(F32).astype(BF16)
        for r in range(nz):
            turned = nt(eye, cust_ref[r])
            w_ref[0:width, r * cols:(r + 1) * cols] = turned.astype(BF16)
            turned_ref[:, r * cols:(r + 1) * cols] = turned.astype(BF16)
            hq_ref[r:r + 1, :] = 0.5 * jnp.sum(turned * turned, axis=0, keepdims=True)
    else:
        w_ref[0:width, :] = turned_ref[...]
    wt = wt_ref[...]
    lam = lam_ref[...]
    a1, a2, a3 = split3(64.0 * lam - hq_ref[...])
    one_c = jnp.ones((3, cols), F32)
    top = (lax.broadcasted_iota(jnp.int32, (16, 128), 0) == 0).astype(F32).astype(BF16)
    for r in range(nz):
        row = slice(r, r + 1)
        at = slice(r * cols, (r + 1) * cols)
        mw = jnp.broadcast_to(-64.0 * wt[row], (3, cols))
        aug = jnp.concatenate([a1[row].astype(F32), a2[row].astype(F32), a3[row].astype(F32), one_c, mw, jnp.zeros((7, cols), F32)], axis=0)
        w_ref[width:width + 16, at] = aug.astype(BF16)
        wrows = jnp.concatenate([wt[row], jnp.zeros((15, cols), F32)], axis=0).astype(BF16)
        d_ref[at, :] = tn(wrows, top).astype(BF16)
    w_ref[width + 16:, :] = jnp.zeros((width - 16, total), BF16)
    cov_ref[...] = jnp.zeros_like(cov_ref)
    soft_ref[...] = jnp.zeros_like(soft_ref)
    lane = lax.broadcasted_iota(jnp.int32, (ROWS, width), 1)
    pad = jnp.where(lane == 3, -30000.0, 0.0).astype(BF16)
    sel = (lax.broadcasted_iota(jnp.int32, (16, width), 0) == lax.broadcasted_iota(jnp.int32, (16, width), 1)).astype(F32).astype(BF16)
    offs = []
    off = jnp.int32(0)
    one_r = jnp.ones((3, n), F32)
    if not first:
        a_ref[:, 0:width] = coords_ref[...]
    for s in range(ny):
        valid = infos_ref[s, 0:1, :]
        if first:
            mu = infos_ref[s, 2:3, :] * valid
            mu_out_ref[s:s + 1, :] = mu
        else:
            mu = mu_ref[s:s + 1, :]
        b = jnp.where(valid > 0, infos_ref[s, 1:2, :], -30000.0)
        parts = [p.astype(F32) for p in split3(b) + split3(mu)]
        rows = jnp.concatenate([one_r] + parts + [jnp.zeros((7, n), F32)], axis=0).astype(BF16)
        side = tn(rows, sel).astype(BF16)
        count = jnp.sum(valid).astype(jnp.int32)
        off = pl.multiple_of(off, ALIGN)
        offs.append(off)
        if first:
            a_ref[pl.ds(off, n), 0:width] = facs_ref[s]
        a_ref[pl.ds(off, n), width:2 * width] = side
        off = off + ((count + ALIGN - 1) // ALIGN) * ALIGN
    tail = pl.multiple_of(off, ALIGN)
    if first:
        a_ref[pl.ds(tail, ROWS), 0:width] = jnp.zeros((ROWS, width), BF16)
    a_ref[pl.ds(tail, ROWS), width:2 * width] = pad
    if first:
        coords_ref[...] = a_ref[:, 0:width]
    n_blocks = (off + ROWS - 1) // ROWS
    scale = math.log2(math.e) / 6.4
    half = tiles // 2

    def dot(base, t, slot):
        y_ref[slot] = jnp.dot(a_ref[pl.ds(base, ROWS), :], w_ref[:, t * BLOCK:(t + 1) * BLOCK], preferred_element_type=F32)

    def weigh(h):
        return jnp.dot(x_ref[h], d_ref[h * half * BLOCK:(h + 1) * half * BLOCK, :], preferred_element_type=F32)

    def body(i, _):
        base = pl.multiple_of(i * ROWS, ROWS)
        acc_ref[pl.ds(base, ROWS), :] = acc_ref[pl.ds(base, ROWS), :] + weigh(1)
        for t in range(tiles):
            if t + 1 < tiles:
                dot(base, t + 1, (t + 1) % 2)
            else:
                dot(pl.multiple_of(base + ROWS, ROWS), 0, (t + 1) % 2)
            for q in range(BLOCK // 128):
                at = slice(t * BLOCK + q * 128, t * BLOCK + (q + 1) * 128)
                xat = slice((t % half) * BLOCK + q * 128, (t % half) * BLOCK + (q + 1) * 128)
                cov = cov_ref[:, at]
                soft = soft_ref[:, at]
                for r in range(0, ROWS, 64):
                    es = [jnp.exp2(y_ref[t % 2, r + 16 * s:r + 16 * s + 16, q * 128:(q + 1) * 128] * scale) for s in range(4)]
                    us = [1.0 + e for e in es]
                    p01 = us[0] * us[1]
                    p23 = us[2] * us[3]
                    r01 = 1.0 / p01
                    r23 = 1.0 / p23
                    xs = [es[0] * (us[1] * r01), es[1] * (us[0] * r01), es[2] * (us[3] * r23), es[3] * (us[2] * r23)]
                    for s in range(4):
                        x_ref[t // half, r + 16 * s:r + 16 * s + 16, xat] = xs[s].astype(BF16)
                    tot = (xs[0] + xs[1]) + (xs[2] + xs[3])
                    lg = jnp.log(p01 * p23)
                    cov = cov + (tot[0:8] + tot[8:16])
                    soft = soft + (lg[0:8] + lg[8:16])
                cov_ref[:, at] = cov
                soft_ref[:, at] = soft
            if t == half - 1:
                acc_ref[pl.ds(pl.multiple_of(base + ROWS, ROWS), ROWS), :] = weigh(0)
        return 0

    dot(0, 0, 0)
    x_ref[1] = jnp.zeros(x_ref.shape[1:], BF16)
    acc_ref[0:ROWS, :] = jnp.zeros((ROWS, 128), F32)
    lax.fori_loop(0, n_blocks, body, 0)
    end = pl.ds(pl.multiple_of(n_blocks * ROWS, ROWS), ROWS)
    acc_ref[end, :] = acc_ref[end, :] + weigh(1)
    diag = lax.broadcasted_iota(jnp.int32, (128, 128), 0) == lax.broadcasted_iota(jnp.int32, (128, 128), 1)
    for s in range(ny):
        for b in range(n // 128):
            at = pl.ds(pl.multiple_of(offs[s] + (b * 128 + ROWS), ALIGN), 128)
            got = jnp.sum(jnp.where(diag, acc_ref[at, :], 0.0), axis=0, keepdims=True)
            load_ref[s:s + 1, b * 128:(b + 1) * 128] = jnp.where(infos_ref[s, 0:1, b * 128:(b + 1) * 128] > 0, got, 0.0)
    soft = 0.0
    for r in range(nz):
        at = slice(r * cols, (r + 1) * cols)
        cover_ref[r:r + 1, :] = jnp.sum(cov_ref[:, at], axis=0, keepdims=True)
        soft = soft + soft_ref[:, at] * wt[r:r + 1]
    mu_all = mu_out_ref if first else mu_ref
    caps = infos_ref[me_y, 3:4, :]
    mine = jnp.sum(mu_all[pl.ds(me_y, 1), :] * caps)
    owned = jnp.sum(lam_ref[pl.ds(me_z, 1), :] * wt_ref[pl.ds(me_z, 1), :])
    here = owned - TAU * jnp.sum(soft) - jnp.where(c == 0, mine, 0.0)
    spot = (lax.broadcasted_iota(jnp.int32, (8, 128), 1) == step) & (lax.broadcasted_iota(jnp.int32, (8, 128), 0) == 0)
    tot_ref[...] = ext_ref[...] + jnp.where(spot, here, 0.0)


def reduce_kernel(step, ny, nc, refs):
    last = step == ITERS - 1
    if last:
        (load_ref, cover_ref, lam_ref, wt_ref, mu_ref, infos_ref, tot_ref,
         lam_out_ref, mu_out_ref, tot_out_ref,
         gotz, gotc, goty, mid, sz, rz, sc, rc, sy, ry, gott, gotp, midt, own, st, rt, sp, rp, sl, rl) = refs
    else:
        (load_ref, cover_ref, lam_ref, wt_ref, mu_ref, infos_ref,
         lam_out_ref, mu_out_ref,
         gotz, gotc, goty, mid, sz, rz, sc, rc, sy, ry) = refs
    size = 0.1 / (step + 1)
    y, z, c = spots()
    zp = [(y * NZ + lax.rem(z + d, NZ), c) for d in range(1, NZ)]
    yp = [(lax.rem(y + d, ny) * NZ + z, c) for d in range(1, ny)]
    cp = [(y * NZ + z, lax.rem(c + d, nc)) for d in range(1, nc)]
    plane = [(lax.rem(y + e, ny) * NZ + z, lax.rem(c + d, nc)) for e in range(ny) for d in range(nc) if e + d > 0]
    sync(zp + (plane if last else yp + cp))
    if last:
        ts = [remote(tot_ref, gott.at[z], st.at[d], rt.at[d], peer) for d, peer in enumerate(zp)]
    zs = [remote(cover_ref, gotz.at[z], sz.at[d], rz.at[d], peer) for d, peer in enumerate(zp)]
    cs = [remote(load_ref, gotc.at[c], sc.at[d], rc.at[d], peer) for d, peer in enumerate(cp)]
    gotz[z] = cover_ref[...]
    gotc[c] = load_ref[...]
    for cpy in cs:
        cpy.wait()
    total = gotc[0]
    for k in range(1, nc):
        total = total + gotc[k]
    mid[...] = total
    goty[y] = total
    ys = [remote(mid, goty.at[y], sy.at[d], ry.at[d], peer) for d, peer in enumerate(yp)]
    if last:
        gott[z] = tot_ref[...]
        for cpy in ts:
            cpy.wait()
        total = gott[0]
        for k in range(1, NZ):
            total = total + gott[k]
        midt[...] = total
        gotp[y * nc + c] = total
        ps = [remote(midt, gotp.at[y * nc + c], sp.at[d], rp.at[d], peer) for d, peer in enumerate(plane)]
    for cpy in zs:
        cpy.wait()
    cover = gotz[0]
    for k in range(1, NZ):
        cover = cover + gotz[k]
    lam = lam_ref[...] + size * wt_ref[...] * (1.0 - cover) / (1.0 + cover)
    if last:
        for r in range(NZ):
            own[r] = lam[r:r + 1]
            lam_out_ref[y * NZ + r] = lam[r:r + 1]
        ls = [remote(own, lam_out_ref.at[pl.ds(y * NZ, NZ)], sl.at[d], rl.at[d], peer) for d, peer in enumerate(yp)]
    else:
        lam_out_ref[...] = lam
    for cpy in ys:
        cpy.wait()
    load = goty[0]
    for k in range(1, ny):
        load = load + goty[k]
    for k in range(ny):
        row = slice(k, k + 1)
        valid = infos_ref[k, 0:1, :]
        cap = infos_ref[k, 3:4, :]
        got = load[row]
        mu = jnp.maximum(0.0, mu_ref[row, :] + size * (got - cap) / (got + jnp.where(valid > 0, cap, 1.0)))
        mu_out_ref[row, :] = mu * valid
    if last:
        for cpy in ps:
            cpy.wait()
        total = gotp[0]
        for k in range(1, ny * nc):
            total = total + gotp[k]
        tot_out_ref[...] = total
        for cpy in ls:
            cpy.wait()


def finish_kernel(total_cust, mu_ref, tot_ref, open_ref, shut_ref, out_ref, bound_ref):
    n = open_ref.shape[1]
    y, z, c = spots()
    rows = jnp.concatenate([v.astype(F32) for v in split3(mu_ref[pl.ds(y, 1), :])] + [jnp.zeros((13, n), F32)], axis=0).astype(BF16)
    got = jnp.dot(rows, onehot_of(open_ref[...]), preferred_element_type=F32)
    out_ref[...] = jnp.where(open_ref[...] > 0, got[0:1] + got[1:2] + got[2:3], shut_ref[...])
    bound_ref[...] = tot_ref[0:1, :] / total_cust


def params(cid=None, mib=24):
    return pltpu.CompilerParams(collective_id=cid, has_side_effects=True, vmem_limit_bytes=mib * 2 ** 20) if cid is not None else pltpu.CompilerParams(vmem_limit_bytes=mib * 2 ** 20)


def packed(kernel, *head):
    def run(*refs):
        kernel(*head, refs)
    return run


def local(nf, nc, fac_coords, cust_coords, open_flags, demand, fixed_cost, capacity, cap_mult, cover_mult):
    n, width = fac_coords.shape
    cols = cust_coords.shape[0]
    ny = nf // NZ
    total_cust = cols * nf * nc
    sd = jax.ShapeDtypeStruct
    dma = pltpu.SemaphoreType.DMA
    scr = pltpu.VMEM
    open_row = open_flags.reshape(1, n)
    comp, info, wt, lam, ext, shut = pl.pallas_call(
        pre_kernel,
        out_shape=(sd((n, width), BF16), sd((8, n), F32), sd((NZ, cols), F32), sd((NZ, cols), F32), sd((8, 128), F32), sd((1, n), F32)),
        in_specs=[VMEM] * 7, out_specs=(VMEM,) * 6, compiler_params=params(), name="pre",
    )(open_row, fac_coords, capacity.reshape(1, n), cap_mult.reshape(1, n), fixed_cost.reshape(1, n),
      demand.reshape(1, nf * cols), cover_mult.reshape(1, nf * cols))
    hops = NZ // 2
    cust, facs, infos = pl.pallas_call(
        functools.partial(gather_kernel, ny),
        out_shape=(sd((NZ, cols, width), BF16), sd((ny, n, width), BF16), sd((ny, 8, n), F32)),
        in_specs=[VMEM] * 3, out_specs=(VMEM,) * 3,
        scratch_shapes=[dma((2, hops, CHUNKS)), dma((2, hops, CHUNKS)), dma((ny - 1, 2)), dma((ny - 1, 2))],
        compiler_params=params(0), name="gather",
    )(cust_coords, comp, info)
    rows = ny * n + 3 * ROWS
    total = NZ * cols
    half = total // BLOCK // 2
    work = [
        scr((rows, 2 * width), BF16),
        scr((2 * width, total), BF16),
        scr((2, ROWS, BLOCK), F32),
        scr((2, ROWS, half * BLOCK), BF16),
        scr((total, 128), BF16),
        scr((rows + n, 128), F32),
        scr((8, total), F32),
        scr((8, total), F32),
    ]
    tot = ext
    mu = None
    for step in range(ITERS):
        last = step == ITERS - 1
        outs = (sd((ny, n), F32), sd((NZ, cols), F32), sd((8, 128), F32))
        if step == 0:
            load, cover, tot, mu, coords, turned, hq = pl.pallas_call(
                packed(step_kernel, step, ny),
                out_shape=outs + (sd((ny, n), F32), sd((rows, width), BF16), sd((width, total), BF16), sd((NZ, cols), F32)),
                in_specs=[VMEM] * 6, out_specs=(VMEM,) * 7, scratch_shapes=work, compiler_params=params(), name="step",
            )(facs, infos, cust, lam, wt, tot)
        else:
            load, cover, tot = pl.pallas_call(
                packed(step_kernel, step, ny),
                out_shape=outs, in_specs=[VMEM] * 8, out_specs=(VMEM,) * 3, scratch_shapes=work,
                compiler_params=params(), name="step",
            )(coords, infos, turned, hq, mu, lam, wt, tot)
        scratch = [scr((NZ, NZ, cols), F32), scr((nc, ny, n), F32), scr((ny, ny, n), F32), scr((ny, n), F32),
                   dma((NZ - 1,)), dma((NZ - 1,)), dma((nc - 1,)), dma((nc - 1,)), dma((ny - 1,)), dma((ny - 1,))]
        if not last:
            lam, mu = pl.pallas_call(
                packed(reduce_kernel, step, ny, nc),
                out_shape=(sd((NZ, cols), F32), sd((ny, n), F32)), in_specs=[VMEM] * 6, out_specs=(VMEM,) * 2,
                scratch_shapes=scratch, compiler_params=params(1 + step), name="reduce",
            )(load, cover, lam, wt, mu, infos)
        else:
            plane = ny * nc
            lam_all, mu, tot = pl.pallas_call(
                packed(reduce_kernel, step, ny, nc),
                out_shape=(sd((nf, 1, cols), F32), sd((ny, n), F32), sd((8, 128), F32)), in_specs=[VMEM] * 7, out_specs=(VMEM,) * 3,
                scratch_shapes=scratch + [scr((NZ, 8, 128), F32), scr((plane, 8, 128), F32), scr((8, 128), F32), scr((NZ, 1, cols), F32),
                                          dma((NZ - 1,)), dma((NZ - 1,)), dma((plane - 1,)), dma((plane - 1,)), dma((ny - 1,)), dma((ny - 1,))],
                compiler_params=params(1 + step), name="reduce",
            )(load, cover, lam, wt, mu, infos, tot)
    cap_final, bounds = pl.pallas_call(
        functools.partial(finish_kernel, total_cust), out_shape=(sd((1, n), F32), sd((1, 128), F32)),
        in_specs=[VMEM] * 4, out_specs=(VMEM,) * 2, compiler_params=params(), name="finish",
    )(mu, tot, open_row, shut)
    return lam_all.reshape(nf * cols), cap_final.reshape(n), bounds[0, :ITERS]


def solution(mesh):
    nf, nc = mesh.shape["fac"], mesh.shape["cust"]
    return jax.shard_map(
        functools.partial(local, nf, nc),
        mesh=mesh,
        in_specs=(P("fac", None), P(("cust", "fac"), None), P("fac"), P("cust"), P("fac"), P("fac"), P("fac"), P("cust")),
        out_specs=(P("cust"), P("fac"), P()),
        check_vma=False,
    )
```

time: 385 us -> 106 us (0.28)
  Pallas kernels: 379 us -> 101 us
    pallas_call x8, Pallas kernels: 377 us -> 99.6 us  [the longest x2 24.7 us: local(): pl.pallas_call(packed(step_kernel, step, ny), out_shape=outs, in_specs=[V...]
where the time goes in v1:
time: 106 us
  Pallas kernels  101 us (95%)
  local copies, waits for them, and re-layouts  4.62 us (4%)
    pallas_call x2, Pallas kernels, local(): pl.pallas_call(packed(step_kernel, step, ny), out_shape=outs, in_specs=[V...  24.7 us
    pallas_call x2, Pallas kernels, local(): pl.pallas_call(packed(reduce_kernel, step, ny, nc), out_shape=(sd((NZ, co...  23.9 us
    pallas_call x1, Pallas kernels, local(): pl.pallas_call(functools.partial(gather_kernel, ny), out_shape=(sd((NZ, c...  21.1 us
    pallas_call x1, Pallas kernels, local(): pl.pallas_call(packed(reduce_kernel, step, ny, nc), out_shape=(sd((nf, 1,...  16.4 us
    pallas_call x1, Pallas kernels, local(): pl.pallas_call(packed(step_kernel, step, ny), out_shape=outs + (sd((ny, n...  12.7 us
    unnamed x17, local copies, waits for them, and re-layouts  4.11 us

profile of v1, /device:TPU:1, one launch (start us, length us, event | category | flops | bytes accessed | tf_op | source)
XLA Modules:
  0.0 105.9 jit_solution(8673408826449017703)
XLA Ops:
  0.6 0.0 copy-start.7
  0.6 0.0 copy-start.6
  0.7 0.0 copy-start.5
  0.7 0.0 copy-start.4
  0.7 0.6 copy-done.7
  1.3 0.0 copy-done.6
  1.3 0.0 copy-done.5
  1.3 0.0 copy-done.4
  1.4 0.0 copy-start
  1.4 0.9 copy-done
  2.3 0.0 copy-start.2
  2.3 0.8 copy-done.2
  3.1 0.0 copy-start.3
  3.1 0.8 copy-done.3
  3.9 0.0 copy-start.1
  4.0 0.7 pre.1
  4.7 0.2 copy-done.1
  4.9 21.1 %gather.1 = (bf16[8,512,128]{2,1,0:T(8,128)(2,1)S(1)}, bf16[4,512,128]{2,1,0:T(8,128)(2,1)S(1)}, f32[4,8,512]{2,1,0:T(8,128)S(1)}) custom-call(bf16[512,128]{1,0:T(8,128)(2,1)S(1)} %copy-done.1, bf16[512,128]{1,0:T(8,128)(2,1)S(1)} %get-tuple-element.34.comp_ref, f32[8,512]{1,0:T(8,128)S(1)} %get-tuple-element.35.info_ref), custom_call_target="tpu_custom_call" | custom-call | tf_op jit(solution)/shard_map/gather/pallas_call | solution.py:401
  25.9 12.7 %step.3 = (f32[4,512]{1,0:T(4,128)S(1)}, f32[8,512]{1,0:T(8,128)S(1)}, f32[8,128]{1,0:T(8,128)S(1)}, f32[4,512]{1,0:T(4,128)S(1)}, bf16[2432,128]{1,0:T(8,128)(2...) custom-call(bf16[4,512,128]{2,1,0:T(8,128)(2,1)S(1)} %get-tuple-element.36.refs_0_, ...), custom_call_target="tpu_custom_call" | custom-call | tf_op jit(solution)/shard_map/step/pallas_call | solution.py:427
  38.7 14.1 %reduce.3 = (f32[8,512]{1,0:T(8,128)S(1)}, f32[4,512]{1,0:T(4,128)S(1)}) custom-call(f32[4,512]{1,0:T(4,128)S(1)} %get-tuple-element.45.refs_0_, f32[8,512]{1,0:T(8,128)S(1)} %get-tuple-element.46.refs_1_, f32[8,512]{1,0:T(8,128)S(1)} %get-tuple-element.39.refs_3_.refs_2_, f32[8,512]{1,0:T(8,128)S(1)} %get-tuple-element.40.refs_4_.refs_3_.refs_6_, ...), custom_call_target="tpu_custom_call" | custom-call | tf_op jit(solution)/shard_map/reduce/pallas_call | solution.py:441
  52.8 12.4 %step.4 = (f32[4,512]{1,0:T(4,128)S(1)}, f32[8,512]{1,0:T(8,128)S(1)}, f32[8,128]{1,0:T(8,128)S(1)}) custom-call(bf16[2432,128]{1,0:T(8,128)(2,1)S(1)} %get-tuple-element.42.refs_0_, f32[4,8,512]{2,1,0:T(8,128)S(1)} %get-tuple-element.37.refs_1_.refs_5_, bf16[128,4096]{1,0:T(8,128)(2,1)S(1)} %get-tuple-element.43.refs_2_, ...), custom_call_target="tpu_custom_call" | custom-call | tf_op jit(solution)/shard_map/step/pallas_call | solution.py:433
  65.2 9.8 %reduce.4 = (f32[8,512]{1,0:T(8,128)S(1)}, f32[4,512]{1,0:T(4,128)S(1)}) custom-call(f32[4,512]{1,0:T(4,128)S(1)} %get-tuple-element.51.refs_0_, f32[8,512]{1,0:T(8,128)S(1)} %get-tuple-element.52.refs_1_, f32[8,512]{1,0:T(8,128)S(1)} %get-tuple-element.49.refs_5_.refs_2_, f32[8,512]{1,0:T(8,128)S(1)} %get-tuple-element.40.refs_4_.refs_3_.refs_6_, ...), custom_call_target="tpu_custom_call" | custom-call | tf_op jit(solution)/shard_map/reduce/pallas_call | solution.py:441
  75.0 12.4 %step.5 = (f32[4,512]{1,0:T(4,128)S(1)}, f32[8,512]{1,0:T(8,128)S(1)}, f32[8,128]{1,0:T(8,128)S(1)}) custom-call(bf16[2432,128]{1,0:T(8,128)(2,1)S(1)} %get-tuple-element.42.refs_0_, f32[4,8,512]{2,1,0:T(8,128)S(1)} %get-tuple-element.37.refs_1_.refs_5_, bf16[128,4096]{1,0:T(8,128)(2,1)S(1)} %get-tuple-element.43.refs_2_, ...), custom_call_target="tpu_custom_call" | custom-call | tf_op jit(solution)/shard_map/step/pallas_call | solution.py:433
  87.3 16.4 %reduce.5 = (f32[32,1,512]{2,1,0:T(1,128)S(1)}, f32[4,512]{1,0:T(4,128)S(1)}, f32[8,128]{1,0:T(8,128)S(1)}) custom-call(f32[4,512]{1,0:T(4,128)S(1)} %get-tuple-element.56.refs_0_, f32[8,512]{1,0:T(8,128)S(1)} %get-tuple-element.57.refs_1_, f32[8,512]{1,0:T(8,128)S(1)} %get-tuple-element.54.refs_5_.refs_2_, ...), custom_call_target="tpu_custom_call" | custom-call | tf_op jit(solution)/shard_map/reduce/pallas_call | solution.py:448
  103.7 1.0 finish.1
  104.7 0.5 slice_bitcast_fusion
  105.2 0.6 copy.12
Async XLA Ops:
  0.6 0.7 copy-start.7
  0.6 0.7 copy-start.6
  0.7 0.7 copy-start.5
  0.7 0.7 copy-start.4
  1.4 0.9 copy-start
  2.3 0.8 copy-start.2
  3.1 0.8 copy-start.3
  3.9 0.9 copy-start.1

commit v2 on v1

v2 whole, which is shorter than its diff:
```python
import functools
import math

import jax
import jax.numpy as jnp
from jax import lax
from jax.experimental import pallas as pl
from jax.experimental.pallas import tpu as pltpu
from jax.sharding import PartitionSpec as P

MESH = pl.DeviceIdType.MESH
ITERS = 3
TAU = 0.1
ALIGN = 16
ROWS = 160
BLOCK = 512
CHUNKS = 4
NZ = 8
F32 = jnp.float32
BF16 = jnp.bfloat16
VMEM = pl.BlockSpec(memory_space=pltpu.VMEM)


def split3(v):
    a = v.astype(BF16)
    r = v - a.astype(F32)
    b = r.astype(BF16)
    c = (r - b.astype(F32)).astype(BF16)
    return a, b, c


def onehot_of(open_row):
    n = open_row.shape[1]
    flags = jnp.broadcast_to(open_row.astype(F32), (16, n)).astype(BF16)
    tri = (lax.broadcasted_iota(jnp.int32, (n, n), 0) <= lax.broadcasted_iota(jnp.int32, (n, n), 1)).astype(F32).astype(BF16)
    pos = jnp.dot(flags, tri, preferred_element_type=F32)[0:1]
    pos = jnp.where(open_row > 0, pos - 1.0, -1.0).astype(jnp.int32)
    hit = lax.broadcasted_iota(jnp.int32, (n, n), 0) == pos
    return jnp.where(hit, 1.0, 0.0).astype(BF16)


def nt(a, b):
    return lax.dot_general(a, b, (((1,), (1,)), ((), ())), preferred_element_type=F32)


def tn(a, b):
    return lax.dot_general(a, b, (((0,), (0,)), ((), ())), preferred_element_type=F32)


def spots():
    f, c = lax.axis_index("fac"), lax.axis_index("cust")
    return f // NZ, lax.rem(f, NZ), c


def sync(peers):
    barrier = pltpu.get_barrier_semaphore()
    for peer in peers:
        pl.semaphore_signal(barrier, inc=1, device_id=peer, device_id_type=MESH)
    pl.semaphore_wait(barrier, len(peers))


def remote(src, dst, send, recv, peer):
    cpy = pltpu.make_async_remote_copy(src, dst, send, recv, device_id=peer, device_id_type=MESH)
    cpy.start()
    return cpy


def compact(opened, fac, mu, cap):
    n, width = fac.shape
    hot = onehot_of(opened)
    comp = jnp.dot(hot, fac, preferred_element_type=F32).astype(BF16)
    sq = fac.astype(F32) ** 2
    s1, s2, _ = split3(sq)
    ones = jnp.ones((16, width), BF16)
    half = -0.5 * (nt(ones, s1) + nt(ones, s2))[0:1]
    rows = [jnp.ones((1, n), BF16)]
    for v in (half, mu, cap):
        rows.extend(split3(v))
    rows = [r.astype(F32) for r in rows] + [jnp.zeros((6, n), F32)]
    got = nt(jnp.concatenate(rows, axis=0).astype(BF16), hot)
    rows = [got[0:1]] + [got[3 * m + 1:3 * m + 2] + got[3 * m + 2:3 * m + 3] + got[3 * m + 3:3 * m + 4] for m in range(3)]
    return comp, jnp.concatenate(rows + [jnp.zeros((4, n), F32)], axis=0)


def gather_kernel(ny, cust_ref, open_ref, fac_ref, cap_ref, mu_ref, fixed_ref, demand_ref, cover_ref,
                  all_ref, facs_ref, infos_ref, wt_ref, lam_ref, ext_ref, shut_ref, sz, rz, sy, ry):
    y, z, c = spots()
    nz, cols = wt_ref.shape
    hops = NZ // 2
    zp = [(y * NZ + lax.rem(z + s, NZ), c) for s in (1, NZ - 1)]
    yp = [(lax.rem(y + d, ny) * NZ + z, c) for d in range(1, ny)]
    part = cols // CHUNKS
    sync(zp + yp)

    def move(d, s, j):
        src = lax.rem(z + (NZ - s if d == 0 else s), NZ)
        at = pl.ds(j * part, part)
        a = cust_ref.at[at] if s == 0 else all_ref.at[src, at]
        return remote(a, all_ref.at[src, at], sz.at[d, s, j], rz.at[d, s, j], zp[d])

    def valid(d, s, j):
        return s < hops - 1 or (s == hops - 1 and (j < CHUNKS // 2) == (d == 0))

    ring = {}
    for j in range(CHUNKS):
        for d in range(2):
            if valid(d, 0, j):
                ring[d, 0, j] = move(d, 0, j)
    comp, info = compact(open_ref[...], fac_ref[...], mu_ref[...], cap_ref[...])
    facs_ref[y] = comp
    infos_ref[y] = info
    for r in range(nz):
        mine = pl.ds(pl.multiple_of((y * nz + r) * cols, cols), cols)
        wt_ref[r:r + 1, :] = demand_ref[:, mine].astype(F32)
        lam_ref[r:r + 1, :] = cover_ref[:, mine]
    opened = open_ref[...].astype(F32)
    shut = mu_ref[...]
    ext = jnp.zeros((1, 128), F32)
    lane = lax.broadcasted_iota(jnp.int32, (1, 128), 1)
    for k in range(ITERS):
        fixed = jnp.sum(opened * fixed_ref[...] - (1.0 - opened) * shut * cap_ref[...])
        ext = ext + jnp.where((lane == k) & (c == 0), fixed, 0.0)
        shut = jnp.maximum(0.0, shut - 0.1 / (k + 1))
    ext_ref[...] = ext
    shut_ref[...] = shut
    all_ref[z] = cust_ref[...]
    side = []
    for k, peer in enumerate(yp):
        side.append(remote(infos_ref.at[y], infos_ref.at[y], sy.at[k, 0], ry.at[k, 0], peer))
        side.append(remote(facs_ref.at[y], facs_ref.at[y], sy.at[k, 1], ry.at[k, 1], peer))
    for s in range(hops):
        for j in range(CHUNKS):
            for d in range(2):
                if valid(d, s, j):
                    ring[d, s, j].wait_recv()
                    if valid(d, s + 1, j):
                        ring[d, s + 1, j] = move(d, s + 1, j)
    for cpy in ring.values():
        cpy.wait_send()
    for cpy in side:
        cpy.wait()


def step_kernel(step, ny, refs):
    first = step == 0
    if first:
        (facs_ref, infos_ref, cust_ref, lam_ref, wt_ref, ext_ref,
         load_ref, cover_ref, tot_ref, mu_out_ref, coords_ref, turned_ref, hq_ref,
         a_ref, w_ref, y_ref, acc_ref, cov_ref, soft_ref, dw_ref, z_ref) = refs
    else:
        (coords_ref, infos_ref, turned_ref, hq_ref, mu_ref, lam_ref, wt_ref, ext_ref,
         load_ref, cover_ref, tot_ref,
         a_ref, w_ref, y_ref, acc_ref, cov_ref, soft_ref, dw_ref, z_ref) = refs
    n = infos_ref.shape[2]
    nz, cols = lam_ref.shape
    width = coords_ref.shape[1]
    total = nz * cols
    tiles = total // BLOCK
    me_y, me_z, c = spots()
    if first:
        eye = (lax.broadcasted_iota(jnp.int32, (width, width), 0) == lax.broadcasted_iota(jnp.int32, (width, width), 1)).astype(F32).astype(BF16)
        for r in range(nz):
            turned = nt(eye, cust_ref[r])
            w_ref[r, 0:width, :] = turned.astype(BF16)
            turned_ref[r] = turned.astype(BF16)
            hq_ref[r:r + 1, :] = 0.5 * jnp.sum(turned * turned, axis=0, keepdims=True)
    else:
        w_ref[:, 0:width, :] = turned_ref[...]
    wt = wt_ref[...]
    lam = lam_ref[...]
    a1, a2, a3 = split3(64.0 * lam - hq_ref[...])
    one_c = jnp.ones((3, cols), F32)
    for r in range(nz):
        row = slice(r, r + 1)
        at = slice(r * cols, (r + 1) * cols)
        mw = jnp.broadcast_to(-64.0 * wt[row], (3, cols))
        aug = jnp.concatenate([a1[row].astype(F32), a2[row].astype(F32), a3[row].astype(F32), one_c, mw, jnp.zeros((7, cols), F32)], axis=0)
        w_ref[r, width:width + 16, :] = aug.astype(BF16)
        dw_ref[:, at] = jnp.broadcast_to(wt[row], (8, cols))
    w_ref[:, width + 16:, :] = jnp.zeros((nz, width - 16, cols), BF16)
    cov_ref[...] = jnp.zeros_like(cov_ref)
    soft_ref[...] = jnp.zeros_like(soft_ref)
    lane = lax.broadcasted_iota(jnp.int32, (ROWS, width), 1)
    pad = jnp.where(lane == 3, -30000.0, 0.0).astype(BF16)
    sel = (lax.broadcasted_iota(jnp.int32, (16, width), 0) == lax.broadcasted_iota(jnp.int32, (16, width), 1)).astype(F32).astype(BF16)
    offs = []
    off = jnp.int32(0)
    one_r = jnp.ones((3, n), F32)
    if not first:
        a_ref[:, 0:width] = coords_ref[...]
    for s in range(ny):
        valid = infos_ref[s, 0:1, :]
        if first:
            mu = infos_ref[s, 2:3, :] * valid
            mu_out_ref[s:s + 1, :] = mu
        else:
            mu = mu_ref[s:s + 1, :]
        b = jnp.where(valid > 0, infos_ref[s, 1:2, :], -30000.0)
        parts = [p.astype(F32) for p in split3(b) + split3(mu)]
        rows = jnp.concatenate([one_r] + parts + [jnp.zeros((7, n), F32)], axis=0).astype(BF16)
        side = tn(rows, sel).astype(BF16)
        count = jnp.sum(valid).astype(jnp.int32)
        off = pl.multiple_of(off, ALIGN)
        offs.append(off)
        if first:
            a_ref[pl.ds(off, n), 0:width] = facs_ref[s]
        a_ref[pl.ds(off, n), width:2 * width] = side
        off = off + ((count + ALIGN - 1) // ALIGN) * ALIGN
    tail = pl.multiple_of(off, ALIGN)
    if first:
        a_ref[pl.ds(tail, ROWS), 0:width] = jnp.zeros((ROWS, width), BF16)
    a_ref[pl.ds(tail, ROWS), width:2 * width] = pad
    if first:
        coords_ref[...] = a_ref[:, 0:width]
    n_blocks = (off + ROWS - 1) // ROWS
    scale = math.log2(math.e) / 6.4

    def dot(base, t, out):
        out[t] = jnp.dot(a_ref[pl.ds(base, ROWS), :], w_ref[t], preferred_element_type=F32)

    def phase(i, cur, nxt):
        base = pl.multiple_of(i * ROWS, ROWS)
        for t in range(tiles):
            dot(pl.multiple_of(base + ROWS, ROWS), t, nxt)
            spans = [slice(t * BLOCK + q * 128, t * BLOCK + (q + 1) * 128) for q in range(BLOCK // 128)]
            covs = [cov_ref[:, at] for at in spans]
            softs = [soft_ref[:, at] for at in spans]
            for r in range(0, ROWS, 32):
                slots = [pl.ds(pl.multiple_of(base + (r + 8 * s), 8), 8) for s in range(4)]
                loads = [acc_ref[at, :] for at in slots] if t else [jnp.zeros((8, 128), F32)] * 4
                for q in range(BLOCK // 128):
                    dw = dw_ref[:, spans[q]]
                    es = [jnp.exp2(cur[t, r + 8 * s:r + 8 * s + 8, q * 128:(q + 1) * 128] * scale) for s in range(4)]
                    us = [1.0 + e for e in es]
                    p01 = us[0] * us[1]
                    p23 = us[2] * us[3]
                    r01 = dw / p01
                    r23 = dw / p23
                    xs = [es[0] * (us[1] * r01), es[1] * (us[0] * r01), es[2] * (us[3] * r23), es[3] * (us[2] * r23)]
                    loads = [a + x for a, x in zip(loads, xs)]
                    covs[q] = covs[q] + ((xs[0] + xs[1]) + (xs[2] + xs[3]))
                    softs[q] = softs[q] + jnp.log(p01 * p23)
                for s in range(4):
                    acc_ref[slots[s], :] = loads[s]
            for q in range(BLOCK // 128):
                cov_ref[:, spans[q]] = covs[q]
                soft_ref[:, spans[q]] = softs[q]

    def body(i, _):
        phase(2 * i, y_ref, z_ref)
        pl.when(2 * i + 1 < n_blocks)(lambda: phase(2 * i + 1, z_ref, y_ref))
        return 0

    for t in range(tiles):
        dot(0, t, y_ref)
    lax.fori_loop(0, (n_blocks + 1) // 2, body, 0)
    ones = jnp.ones((16, 128), BF16)
    for s in range(ny):
        for b in range(n // 128):
            at = pl.ds(pl.multiple_of(offs[s] + b * 128, ALIGN), 128)
            got = sum(nt(ones, p)[0:1] for p in split3(acc_ref[at, :]))
            load_ref[s:s + 1, b * 128:(b + 1) * 128] = jnp.where(infos_ref[s, 0:1, b * 128:(b + 1) * 128] > 0, got, 0.0)
    soft = 0.0
    for r in range(nz):
        at = slice(r * cols, (r + 1) * cols)
        cover_ref[r:r + 1, :] = jnp.sum(cov_ref[:, at], axis=0, keepdims=True) / wt[r:r + 1]
        soft = soft + soft_ref[:, at] * wt[r:r + 1]
    mu_all = mu_out_ref if first else mu_ref
    caps = infos_ref[me_y, 3:4, :]
    mine = jnp.sum(mu_all[pl.ds(me_y, 1), :] * caps)
    owned = jnp.sum(lam_ref[pl.ds(me_z, 1), :] * wt_ref[pl.ds(me_z, 1), :])
    here = owned - TAU * jnp.sum(soft) - jnp.where(c == 0, mine, 0.0)
    spot = lax.broadcasted_iota(jnp.int32, (1, 128), 1) == step
    tot_ref[...] = ext_ref[...] + jnp.where(spot, here, 0.0)


def far(n):
    return sorted(range(1, n), key=lambda d: -min(d, n - d))


def reduce_kernel(step, ny, nc, refs):
    last = step == ITERS - 1
    if last:
        (load_ref, cover_ref, lam_ref, wt_ref, mu_ref, infos_ref, tot_ref,
         lam_out_ref, mu_out_ref, tot_out_ref,
         gotz, gotc, goty, mid, sz, rz, sc, rc, sy, ry, gott, gotp, midt, own, st, rt, sp, rp, sl, rl) = refs
    else:
        (load_ref, cover_ref, lam_ref, wt_ref, mu_ref, infos_ref,
         lam_out_ref, mu_out_ref,
         gotz, gotc, goty, mid, sz, rz, sc, rc, sy, ry) = refs
    size = 0.1 / (step + 1)
    y, z, c = spots()
    zp = [(y * NZ + lax.rem(z + d, NZ), c) for d in far(NZ)]
    yp = [(lax.rem(y + d, ny) * NZ + z, c) for d in far(ny)]
    cp = [(y * NZ + z, lax.rem(c + d, nc)) for d in far(nc)]
    plane = [(lax.rem(y + e, ny) * NZ + z, lax.rem(c + d, nc)) for e in far(ny) + [0] for d in far(nc) + [0] if e + d > 0]
    sync(zp + (plane if last else yp + cp))
    if last:
        ts = [remote(tot_ref, gott.at[z], st.at[d], rt.at[d], peer) for d, peer in enumerate(zp)]
    zs = [remote(cover_ref, gotz.at[z], sz.at[d], rz.at[d], peer) for d, peer in enumerate(zp)]
    cs = [remote(load_ref, gotc.at[c], sc.at[d], rc.at[d], peer) for d, peer in enumerate(cp)]
    gotz[z] = cover_ref[...]
    gotc[c] = load_ref[...]
    for cpy in cs:
        cpy.wait()
    total = gotc[0]
    for k in range(1, nc):
        total = total + gotc[k]
    mid[...] = total
    goty[y] = total
    ys = [remote(mid, goty.at[y], sy.at[d], ry.at[d], peer) for d, peer in enumerate(yp)]
    if last:
        gott[z] = tot_ref[...]
        for cpy in ts:
            cpy.wait()
        total = gott[0]
        for k in range(1, NZ):
            total = total + gott[k]
        midt[...] = total
        gotp[y * nc + c] = total
        ps = [remote(midt, gotp.at[y * nc + c], sp.at[d], rp.at[d], peer) for d, peer in enumerate(plane)]
    for cpy in zs:
        cpy.wait()
    cover = gotz[0]
    for k in range(1, NZ):
        cover = cover + gotz[k]
    lam = lam_ref[...] + size * wt_ref[...] * (1.0 - cover) / (1.0 + cover)
    if last:
        for r in range(NZ):
            own[r] = lam[r:r + 1]
            lam_out_ref[y * NZ + r] = lam[r:r + 1]
        ls = [remote(own, lam_out_ref.at[pl.ds(y * NZ, NZ)], sl.at[d], rl.at[d], peer) for d, peer in enumerate(yp)]
    else:
        lam_out_ref[...] = lam
    for cpy in ys:
        cpy.wait()
    load = goty[0]
    for k in range(1, ny):
        load = load + goty[k]
    for k in range(ny):
        row = slice(k, k + 1)
        valid = infos_ref[k, 0:1, :]
        cap = infos_ref[k, 3:4, :]
        got = load[row]
        mu = jnp.maximum(0.0, mu_ref[row, :] + size * (got - cap) / (got + jnp.where(valid > 0, cap, 1.0)))
        mu_out_ref[row, :] = mu * valid
    if last:
        for cpy in ps:
            cpy.wait()
        total = gotp[0]
        for k in range(1, ny * nc):
            total = total + gotp[k]
        tot_out_ref[...] = total
        for cpy in ls:
            cpy.wait()


def finish_kernel(total_cust, mu_ref, tot_ref, open_ref, shut_ref, out_ref, bound_ref):
    n = open_ref.shape[1]
    y, z, c = spots()
    rows = jnp.concatenate([v.astype(F32) for v in split3(mu_ref[pl.ds(y, 1), :])] + [jnp.zeros((13, n), F32)], axis=0).astype(BF16)
    got = jnp.dot(rows, onehot_of(open_ref[...]), preferred_element_type=F32)
    out_ref[...] = jnp.where(open_ref[...] > 0, got[0:1] + got[1:2] + got[2:3], shut_ref[...])
    bound_ref[...] = tot_ref[...] / total_cust


def params(cid=None, mib=24):
    return pltpu.CompilerParams(collective_id=cid, has_side_effects=True, vmem_limit_bytes=mib * 2 ** 20) if cid is not None else pltpu.CompilerParams(vmem_limit_bytes=mib * 2 ** 20)


def packed(kernel, *head):
    def run(*refs):
        kernel(*head, refs)
    return run


def work_of(ny, n, cols, width):
    scr = pltpu.VMEM
    rows = ny * n + 3 * ROWS
    total = NZ * cols
    return rows, [
        scr((rows, 2 * width), BF16),
        scr((total // BLOCK, 2 * width, BLOCK), BF16),
        scr((total // BLOCK, ROWS, BLOCK), F32),
        scr((rows, 128), F32),
        scr((8, total), F32),
        scr((8, total), F32),
        scr((8, total), F32),
        scr((total // BLOCK, ROWS, BLOCK), F32),
    ]


def local(nf, nc, fac_coords, cust_coords, open_flags, demand, fixed_cost, capacity, cap_mult, cover_mult):
    n, width = fac_coords.shape
    cols = cust_coords.shape[0]
    ny = nf // NZ
    total_cust = cols * nf * nc
    sd = jax.ShapeDtypeStruct
    dma = pltpu.SemaphoreType.DMA
    scr = pltpu.VMEM
    open_row = open_flags.reshape(1, n)
    hops = NZ // 2
    cust, facs, infos, wt, lam, ext, shut = pl.pallas_call(
        functools.partial(gather_kernel, ny),
        out_shape=(sd((NZ, cols, width), BF16), sd((ny, n, width), BF16), sd((ny, 8, n), F32),
                   sd((NZ, cols), F32), sd((NZ, cols), F32), sd((1, 128), F32), sd((1, n), F32)),
        in_specs=[VMEM] * 8, out_specs=(VMEM,) * 7,
        scratch_shapes=[dma((2, hops, CHUNKS)), dma((2, hops, CHUNKS)), dma((ny - 1, 2)), dma((ny - 1, 2))],
        compiler_params=params(0), name="gather",
    )(cust_coords, open_row, fac_coords, capacity.reshape(1, n), cap_mult.reshape(1, n), fixed_cost.reshape(1, n),
      demand.reshape(1, nf * cols), cover_mult.reshape(1, nf * cols))
    rows, work = work_of(ny, n, cols, width)
    tot = ext
    mu = None
    for step in range(ITERS):
        last = step == ITERS - 1
        outs = (sd((ny, n), F32), sd((NZ, cols), F32), sd((1, 128), F32))
        if step == 0:
            load, cover, tot, mu, coords, turned, hq = pl.pallas_call(
                packed(step_kernel, step, ny),
                out_shape=outs + (sd((ny, n), F32), sd((rows, width), BF16), sd((NZ, width, cols), BF16), sd((NZ, cols), F32)),
                in_specs=[VMEM] * 6, out_specs=(VMEM,) * 7, scratch_shapes=work, compiler_params=params(), name="step",
            )(facs, infos, cust, lam, wt, tot)
        else:
            load, cover, tot = pl.pallas_call(
                packed(step_kernel, step, ny),
                out_shape=outs, in_specs=[VMEM] * 8, out_specs=(VMEM,) * 3, scratch_shapes=work,
                compiler_params=params(), name="step",
            )(coords, infos, turned, hq, mu, lam, wt, tot)
        scratch = [scr((NZ, NZ, cols), F32), scr((nc, ny, n), F32), scr((ny, ny, n), F32), scr((ny, n), F32),
                   dma((NZ - 1,)), dma((NZ - 1,)), dma((nc - 1,)), dma((nc - 1,)), dma((ny - 1,)), dma((ny - 1,))]
        if not last:
            lam, mu = pl.pallas_call(
                packed(reduce_kernel, step, ny, nc),
                out_shape=(sd((NZ, cols), F32), sd((ny, n), F32)), in_specs=[VMEM] * 6, out_specs=(VMEM,) * 2,
                scratch_shapes=scratch, compiler_params=params(1 + step), name="reduce",
            )(load, cover, lam, wt, mu, infos)
        else:
            plane = ny * nc
            lam_all, mu, tot = pl.pallas_call(
                packed(reduce_kernel, step, ny, nc),
                out_shape=(sd((nf, 1, cols), F32), sd((ny, n), F32), sd((1, 128), F32)), in_specs=[VMEM] * 7, out_specs=(VMEM,) * 3,
                scratch_shapes=scratch + [scr((NZ, 1, 128), F32), scr((plane, 1, 128), F32), scr((1, 128), F32), scr((NZ, 1, cols), F32),
                                          dma((NZ - 1,)), dma((NZ - 1,)), dma((plane - 1,)), dma((plane - 1,)), dma((ny - 1,)), dma((ny - 1,))],
                compiler_params=params(1 + step), name="reduce",
            )(load, cover, lam, wt, mu, infos, tot)
    cap_final, bounds = pl.pallas_call(
        functools.partial(finish_kernel, total_cust), out_shape=(sd((1, n), F32), sd((1, 128), F32)),
        in_specs=[VMEM] * 4, out_specs=(VMEM,) * 2, compiler_params=params(), name="finish",
    )(mu, tot, open_row, shut)
    return lam_all.reshape(nf * cols), cap_final.reshape(n), bounds[0, :ITERS]


def solution(mesh):
    nf, nc = mesh.shape["fac"], mesh.shape["cust"]
    return jax.shard_map(
        functools.partial(local, nf, nc),
        mesh=mesh,
        in_specs=(P("fac", None), P(("cust", "fac"), None), P("fac"), P("cust"), P("fac"), P("fac"), P("fac"), P("cust")),
        out_specs=(P("cust"), P("fac"), P()),
        check_vma=False,
    )
```

time: 106 us -> 94.3 us (0.89)
  Pallas kernels: 101 us -> 88 us
    pallas_call x2, Pallas kernels: 24.7 us -> 18.4 us  [local(): pl.pallas_call(packed(step_kernel, step, ny), out_shape=outs, in_specs=[V...]
    pallas_call x1, Pallas kernels: 12.7 us -> 9.54 us  [local(): pl.pallas_call(packed(step_kernel, step, ny), out_shape=outs + (sd((ny, n...]
    pallas_call x1, Pallas kernels: 16.4 us -> 14.2 us  [local(): pl.pallas_call(packed(reduce_kernel, step, ny, nc), out_shape=(sd((nf, 1,...]
where the time goes in v2:
time: 94.3 us; the launch traced here: 94 us
  Pallas kernels  88 us (93%)
  local copies, waits for them, and re-layouts  5.33 us (6%)
    pallas_call x2, Pallas kernels, local(): pl.pallas_call(packed(reduce_kernel, step, ny, nc), out_shape=(sd((NZ, co...  23.8 us
    pallas_call x1, Pallas kernels, local(): pl.pallas_call(functools.partial(gather_kernel, ny), out_shape=(sd((NZ, c...  21.1 us
    pallas_call x2, Pallas kernels, local(): pl.pallas_call(packed(step_kernel, step, ny), out_shape=outs, in_specs=[V...  18.4 us
    pallas_call x1, Pallas kernels, local(): pl.pallas_call(packed(reduce_kernel, step, ny, nc), out_shape=(sd((nf, 1,...  14.2 us
    pallas_call x1, Pallas kernels, local(): pl.pallas_call(packed(step_kernel, step, ny), out_shape=outs + (sd((ny, n...  9.54 us
    unnamed x17, local copies, waits for them, and re-layouts  4.82 us

profile of v2, /device:TPU:1, one launch (start us, length us, event | category | flops | bytes accessed | tf_op | source)
XLA Modules:
  0.0 94.0 jit_solution(17950734583824482319)
XLA Ops:
  0.6 0.0 copy-start.7
  0.6 0.0 copy-start.6
  0.7 0.0 copy-start.5
  0.7 0.0 copy-start.4
  0.7 0.6 copy-done.7
  1.3 0.0 copy-done.6
  1.3 0.0 copy-done.5
  1.3 0.0 copy-done.4
  1.4 0.0 copy-start
  1.4 0.9 copy-done
  2.3 0.0 copy-start.1
  2.3 0.9 copy-done.1
  3.2 0.0 copy-start.2
  3.2 0.8 copy-done.2
  4.0 0.0 copy-start.3
  4.0 0.8 copy-done.3
  4.9 21.1 %gather.1 = (bf16[8,512,128]{2,1,0:T(8,128)(2,1)S(1)}, bf16[4,512,128]{2,1,0:T(8,128)(2,1)S(1)}, f32[4,8,512]{2,1,0:T(8,128)S(1)}, f32[8,512]{1,0:T(8,128)S(1)},...) custom-call(bf16[512,128]{1,0:T(8,128)(2,1)S(1)} %copy-done, s32[1,512]{1,0:T(1,128)S(1)} %bitcast.13, ...), custom_call_target="tpu_custom_call" | custom-call | tf_op jit(solution)/shard_map/gather/pallas_call | solution.py:403
  25.9 9.5 %step.3 = (f32[4,512]{1,0:T(4,128)S(1)}, f32[8,512]{1,0:T(8,128)S(1)}, f32[1,128]{1,0:T(1,128)S(1)}, f32[4,512]{1,0:T(4,128)S(1)}, bf16[2528,128]{1,0:T(8,128)(2...) custom-call(bf16[4,512,128]{2,1,0:T(8,128)(2,1)S(1)} %get-tuple-element.32.refs_0_, ...), custom_call_target="tpu_custom_call" | custom-call | tf_op jit(solution)/shard_map/step/pallas_call | solution.py:419
  35.5 13.9 %reduce.3 = (f32[8,512]{1,0:T(8,128)S(1)}, f32[4,512]{1,0:T(4,128)S(1)}) custom-call(f32[4,512]{1,0:T(4,128)S(1)} %get-tuple-element.41.refs_0_, f32[8,512]{1,0:T(8,128)S(1)} %get-tuple-element.42.refs_1_, f32[8,512]{1,0:T(8,128)S(1)} %get-tuple-element.35.refs_3_.refs_2_, f32[8,512]{1,0:T(8,128)S(1)} %get-tuple-element.36.refs_4_.refs_3_.refs_6_, ...), custom_call_target="tpu_custom_call" | custom-call | tf_op jit(solution)/shard_map/reduce/pallas_call | solution.py:433
  49.4 9.1 %step.4 = (f32[4,512]{1,0:T(4,128)S(1)}, f32[8,512]{1,0:T(8,128)S(1)}, f32[1,128]{1,0:T(1,128)S(1)}) custom-call(bf16[2528,128]{1,0:T(8,128)(2,1)S(1)} %get-tuple-element.38.refs_0_, f32[4,8,512]{2,1,0:T(8,128)S(1)} %get-tuple-element.33.refs_1_.refs_5_, bf16[8,128,512]{2,1,0:T(8,128)(2,1)S(1)} %get-tuple-element.39.refs_2_, ...), custom_call_target="tpu_custom_call" | custom-call | tf_op jit(solution)/shard_map/step/pallas_call | solution.py:425
  58.5 9.9 %reduce.4 = (f32[8,512]{1,0:T(8,128)S(1)}, f32[4,512]{1,0:T(4,128)S(1)}) custom-call(f32[4,512]{1,0:T(4,128)S(1)} %get-tuple-element.47.refs_0_, f32[8,512]{1,0:T(8,128)S(1)} %get-tuple-element.48.refs_1_, f32[8,512]{1,0:T(8,128)S(1)} %get-tuple-element.45.refs_5_.refs_2_, f32[8,512]{1,0:T(8,128)S(1)} %get-tuple-element.36.refs_4_.refs_3_.refs_6_, ...), custom_call_target="tpu_custom_call" | custom-call | tf_op jit(solution)/shard_map/reduce/pallas_call | solution.py:433
  68.4 9.3 %step.5 = (f32[4,512]{1,0:T(4,128)S(1)}, f32[8,512]{1,0:T(8,128)S(1)}, f32[1,128]{1,0:T(1,128)S(1)}) custom-call(bf16[2528,128]{1,0:T(8,128)(2,1)S(1)} %get-tuple-element.38.refs_0_, f32[4,8,512]{2,1,0:T(8,128)S(1)} %get-tuple-element.33.refs_1_.refs_5_, bf16[8,128,512]{2,1,0:T(8,128)(2,1)S(1)} %get-tuple-element.39.refs_2_, ...), custom_call_target="tpu_custom_call" | custom-call | tf_op jit(solution)/shard_map/step/pallas_call | solution.py:425
  77.7 14.2 %reduce.5 = (f32[32,1,512]{2,1,0:T(1,128)S(1)}, f32[4,512]{1,0:T(4,128)S(1)}, f32[1,128]{1,0:T(1,128)S(1)}) custom-call(f32[4,512]{1,0:T(4,128)S(1)} %get-tuple-element.52.refs_0_, f32[8,512]{1,0:T(8,128)S(1)} %get-tuple-element.53.refs_1_, f32[8,512]{1,0:T(8,128)S(1)} %get-tuple-element.50.refs_5_.refs_2_, ...), custom_call_target="tpu_custom_call" | custom-call | tf_op jit(solution)/shard_map/reduce/pallas_call | solution.py:440
  91.9 1.0 %finish.1 = (f32[1,512]{1,0:T(1,128)}, f32[1,128]{1,0:T(1,128)S(1)}) custom-call(f32[4,512]{1,0:T(4,128)S(1)} %get-tuple-element.56.mu_ref, f32[1,128]{1,0:T(1,128)S(1)} %get-tuple-element.57.tot_ref, s32[1,512]{1,0:T(1,128)S(1)} %bitcast.14, f32[1,512]{1,0:T(1,128)S(1)} %get-tuple-element.58.shut_ref), custom_call_target="tpu_custom_call" | custom-call | tf_op jit(solution)/shard_map/finish/pallas_call | solution.py:447
  92.9 0.5 slice_bitcast_fusion
  93.4 0.6 copy.12
Async XLA Ops:
  0.6 0.7 copy-start.7
  0.6 0.7 copy-start.6
  0.7 0.7 copy-start.5
  0.7 0.7 copy-start.4
  1.4 0.9 copy-start
  2.3 0.9 copy-start.1
  3.2 0.8 copy-start.2
  4.0 0.8 copy-start.3

commit v3 on v2

--- a/solution.py
+++ b/solution.py
@@ -14,11 +14,12 @@
 ALIGN = 16
 ROWS = 160
 BLOCK = 512
-CHUNKS = 4
+CHUNKS = 8
 NZ = 8
 F32 = jnp.float32
 BF16 = jnp.bfloat16
 VMEM = pl.BlockSpec(memory_space=pltpu.VMEM)
+HBM = pl.BlockSpec(memory_space=pltpu.HBM)
 
 
 def split3(v):
@@ -82,35 +83,44 @@
     return comp, jnp.concatenate(rows + [jnp.zeros((4, n), F32)], axis=0)
 
 
-def gather_kernel(ny, cust_ref, open_ref, fac_ref, cap_ref, mu_ref, fixed_ref, demand_ref, cover_ref,
-                  all_ref, facs_ref, infos_ref, wt_ref, lam_ref, ext_ref, shut_ref, sz, rz, sy, ry):
+def gather_kernel(ny, cust_hbm, open_hbm, fac_hbm, cap_hbm, mu_hbm, fixed_hbm, demand_hbm, cover_hbm,
+                  all_ref, facs_ref, infos_ref, wt_ref, lam_ref, ext_ref, shut_ref,
+                  open_ref, fac_ref, cap_ref, mu_ref, fixed_ref, demand_ref, cover_ref, sz, rz, sy, ry, loc):
     y, z, c = spots()
     nz, cols = wt_ref.shape
     hops = NZ // 2
     zp = [(y * NZ + lax.rem(z + s, NZ), c) for s in (1, NZ - 1)]
     yp = [(lax.rem(y + d, ny) * NZ + z, c) for d in range(1, ny)]
     part = cols // CHUNKS
+    segment = pl.ds(pl.multiple_of(y * (nz * cols), nz * cols), nz * cols)
+    pairs = [(cust_hbm, all_ref.at[z]), (fac_hbm, fac_ref), (open_hbm, open_ref), (cap_hbm, cap_ref), (mu_hbm, mu_ref),
+             (fixed_hbm, fixed_ref), (demand_hbm.at[:, segment], demand_ref), (cover_hbm.at[:, segment], cover_ref)]
+    own = [pltpu.make_async_copy(a, b, loc.at[k]) for k, (a, b) in enumerate(pairs)]
+    for cpy in own:
+        cpy.start()
     sync(zp + yp)
 
     def move(d, s, j):
         src = lax.rem(z + (NZ - s if d == 0 else s), NZ)
         at = pl.ds(j * part, part)
-        a = cust_ref.at[at] if s == 0 else all_ref.at[src, at]
-        return remote(a, all_ref.at[src, at], sz.at[d, s, j], rz.at[d, s, j], zp[d])
+        return remote(all_ref.at[src, at], all_ref.at[src, at], sz.at[d, s, j], rz.at[d, s, j], zp[d])
 
     def valid(d, s, j):
         return s < hops - 1 or (s == hops - 1 and (j < CHUNKS // 2) == (d == 0))
 
     ring = {}
+    own[0].wait()
     for j in range(CHUNKS):
         for d in range(2):
             if valid(d, 0, j):
                 ring[d, 0, j] = move(d, 0, j)
+    for cpy in own[1:]:
+        cpy.wait()
     comp, info = compact(open_ref[...], fac_ref[...], mu_ref[...], cap_ref[...])
     facs_ref[y] = comp
     infos_ref[y] = info
     for r in range(nz):
-        mine = pl.ds(pl.multiple_of((y * nz + r) * cols, cols), cols)
+        mine = slice(r * cols, (r + 1) * cols)
         wt_ref[r:r + 1, :] = demand_ref[:, mine].astype(F32)
         lam_ref[r:r + 1, :] = cover_ref[:, mine]
     opened = open_ref[...].astype(F32)
@@ -123,7 +133,6 @@
         shut = jnp.maximum(0.0, shut - 0.1 / (k + 1))
     ext_ref[...] = ext
     shut_ref[...] = shut
-    all_ref[z] = cust_ref[...]
     side = []
     for k, peer in enumerate(yp):
         side.append(remote(infos_ref.at[y], infos_ref.at[y], sy.at[k, 0], ry.at[k, 0], peer))
@@ -218,9 +227,11 @@
     def dot(base, t, out):
         out[t] = jnp.dot(a_ref[pl.ds(base, ROWS), :], w_ref[t], preferred_element_type=F32)
 
-    def phase(i, cur, nxt):
+    def phase(i, cur, nxt, opening=False):
         base = pl.multiple_of(i * ROWS, ROWS)
         for t in range(tiles):
+            if opening and t + 1 < tiles:
+                dot(0, t + 1, cur)
             dot(pl.multiple_of(base + ROWS, ROWS), t, nxt)
             spans = [slice(t * BLOCK + q * 128, t * BLOCK + (q + 1) * 128) for q in range(BLOCK // 128)]
             covs = [cov_ref[:, at] for at in spans]
@@ -247,18 +258,18 @@
                 soft_ref[:, spans[q]] = softs[q]
 
     def body(i, _):
-        phase(2 * i, y_ref, z_ref)
-        pl.when(2 * i + 1 < n_blocks)(lambda: phase(2 * i + 1, z_ref, y_ref))
+        phase(2 * i + 1, z_ref, y_ref)
+        pl.when(2 * i + 2 < n_blocks)(lambda: phase(2 * i + 2, y_ref, z_ref))
         return 0
 
-    for t in range(tiles):
-        dot(0, t, y_ref)
-    lax.fori_loop(0, (n_blocks + 1) // 2, body, 0)
+    dot(0, 0, y_ref)
+    phase(jnp.int32(0), y_ref, z_ref, True)
+    lax.fori_loop(0, n_blocks // 2, body, 0)
     ones = jnp.ones((16, 128), BF16)
     for s in range(ny):
         for b in range(n // 128):
             at = pl.ds(pl.multiple_of(offs[s] + b * 128, ALIGN), 128)
-            got = sum(nt(ones, p)[0:1] for p in split3(acc_ref[at, :]))
+            got = sum(nt(ones, p)[0:1] for p in split3(acc_ref[at, :])[:2])
             load_ref[s:s + 1, b * 128:(b + 1) * 128] = jnp.where(infos_ref[s, 0:1, b * 128:(b + 1) * 128] > 0, got, 0.0)
     soft = 0.0
     for r in range(nz):
@@ -281,8 +292,8 @@
 def reduce_kernel(step, ny, nc, refs):
     last = step == ITERS - 1
     if last:
-        (load_ref, cover_ref, lam_ref, wt_ref, mu_ref, infos_ref, tot_ref,
-         lam_out_ref, mu_out_ref, tot_out_ref,
+        (load_ref, cover_ref, lam_ref, wt_ref, mu_ref, infos_ref, tot_ref, open_ref, shut_ref,
+         lam_out_ref, cap_out_ref, bound_ref, mu_out_ref,
          gotz, gotc, goty, mid, sz, rz, sc, rc, sy, ry, gott, gotp, midt, own, st, rt, sp, rp, sl, rl) = refs
     else:
         (load_ref, cover_ref, lam_ref, wt_ref, mu_ref, infos_ref,
@@ -345,23 +356,19 @@
         mu = jnp.maximum(0.0, mu_ref[row, :] + size * (got - cap) / (got + jnp.where(valid > 0, cap, 1.0)))
         mu_out_ref[row, :] = mu * valid
     if last:
+        n = open_ref.shape[1]
+        parts = [v.astype(F32) for v in split3(mu_out_ref[pl.ds(y, 1), :])]
+        rows = jnp.concatenate(parts + [jnp.zeros((13, n), F32)], axis=0).astype(BF16)
+        got = jnp.dot(rows, onehot_of(open_ref[...]), preferred_element_type=F32)
+        cap_out_ref[...] = jnp.where(open_ref[...] > 0, got[0:1] + got[1:2] + got[2:3], shut_ref[...])
         for cpy in ps:
             cpy.wait()
         total = gotp[0]
         for k in range(1, ny * nc):
             total = total + gotp[k]
-        tot_out_ref[...] = total
+        bound_ref[...] = total / (NZ * ny * nc * lam_ref.shape[1])
         for cpy in ls:
             cpy.wait()
-
-
-def finish_kernel(total_cust, mu_ref, tot_ref, open_ref, shut_ref, out_ref, bound_ref):
-    n = open_ref.shape[1]
-    y, z, c = spots()
-    rows = jnp.concatenate([v.astype(F32) for v in split3(mu_ref[pl.ds(y, 1), :])] + [jnp.zeros((13, n), F32)], axis=0).astype(BF16)
-    got = jnp.dot(rows, onehot_of(open_ref[...]), preferred_element_type=F32)
-    out_ref[...] = jnp.where(open_ref[...] > 0, got[0:1] + got[1:2] + got[2:3], shut_ref[...])
-    bound_ref[...] = tot_ref[...] / total_cust
 
 
 def params(cid=None, mib=24):
@@ -394,7 +401,6 @@
     n, width = fac_coords.shape
     cols = cust_coords.shape[0]
     ny = nf // NZ
-    total_cust = cols * nf * nc
     sd = jax.ShapeDtypeStruct
     dma = pltpu.SemaphoreType.DMA
     scr = pltpu.VMEM
@@ -404,11 +410,14 @@
         functools.partial(gather_kernel, ny),
         out_shape=(sd((NZ, cols, width), BF16), sd((ny, n, width), BF16), sd((ny, 8, n), F32),
                    sd((NZ, cols), F32), sd((NZ, cols), F32), sd((1, 128), F32), sd((1, n), F32)),
-        in_specs=[VMEM] * 8, out_specs=(VMEM,) * 7,
-        scratch_shapes=[dma((2, hops, CHUNKS)), dma((2, hops, CHUNKS)), dma((ny - 1, 2)), dma((ny - 1, 2))],
+        in_specs=[HBM] * 8, out_specs=(VMEM,) * 7,
+        scratch_shapes=[scr((1, n), jnp.int32), scr((n, width), BF16), scr((1, n), F32), scr((1, n), F32), scr((1, n), F32),
+                        scr((1, NZ * cols), jnp.int32), scr((1, NZ * cols), F32),
+                        dma((2, hops, CHUNKS)), dma((2, hops, CHUNKS)), dma((ny - 1, 2)), dma((ny - 1, 2)), dma((8,))],
         compiler_params=params(0), name="gather",
-    )(cust_coords, open_row, fac_coords, capacity.reshape(1, n), cap_mult.reshape(1, n), fixed_cost.reshape(1, n),
-      demand.reshape(1, nf * cols), cover_mult.reshape(1, nf * cols))
+    )(*[pltpu.with_memory_space_constraint(v, pltpu.HBM) for v in (
+        cust_coords, open_row, fac_coords, capacity.reshape(1, n), cap_mult.reshape(1, n), fixed_cost.reshape(1, n),
+        demand.reshape(1, nf * cols), cover_mult.reshape(1, nf * cols))])
     rows, work = work_of(ny, n, cols, width)
     tot = ext
     mu = None
@@ -437,17 +446,14 @@
             )(load, cover, lam, wt, mu, infos)
         else:
             plane = ny * nc
-            lam_all, mu, tot = pl.pallas_call(
+            lam_all, cap_final, bounds = pl.pallas_call(
                 packed(reduce_kernel, step, ny, nc),
-                out_shape=(sd((nf, 1, cols), F32), sd((ny, n), F32), sd((1, 128), F32)), in_specs=[VMEM] * 7, out_specs=(VMEM,) * 3,
-                scratch_shapes=scratch + [scr((NZ, 1, 128), F32), scr((plane, 1, 128), F32), scr((1, 128), F32), scr((NZ, 1, cols), F32),
-                                          dma((NZ - 1,)), dma((NZ - 1,)), dma((plane - 1,)), dma((plane - 1,)), dma((ny - 1,)), dma((ny - 1,))],
+                out_shape=(sd((nf, 1, cols), F32), sd((1, n), F32), sd((1, 128), F32)), in_specs=[VMEM] * 9, out_specs=(VMEM,) * 3,
+                scratch_shapes=[scr((ny, n), F32)] + scratch + [
+                    scr((NZ, 1, 128), F32), scr((plane, 1, 128), F32), scr((1, 128), F32), scr((NZ, 1, cols), F32),
+                    dma((NZ - 1,)), dma((NZ - 1,)), dma((plane - 1,)), dma((plane - 1,)), dma((ny - 1,)), dma((ny - 1,))],
                 compiler_params=params(1 + step), name="reduce",
-            )(load, cover, lam, wt, mu, infos, tot)
-    cap_final, bounds = pl.pallas_call(
-        functools.partial(finish_kernel, total_cust), out_shape=(sd((1, n), F32), sd((1, 128), F32)),
-        in_specs=[VMEM] * 4, out_specs=(VMEM,) * 2, compiler_params=params(), name="finish",
-    )(mu, tot, open_row, shut)
+            )(load, cover, lam, wt, mu, infos, tot, open_row, shut)
     return lam_all.reshape(nf * cols), cap_final.reshape(n), bounds[0, :ITERS]
 
 

time: 94.3 us -> 89.4 us (0.948)
  local copies, waits for them, and re-layouts: 5.33 us -> 2.41 us
  Pallas kernels: 88 us -> 86.2 us
    unnamed x17 -> x4, local copies, waits for them, and re-layouts: 4.82 us -> 1.89 us
    pallas_call x1 -> x0, Pallas kernels: 0.97 us -> none  [local(): pl.pallas_call(functools.partial(finish_kernel, total_cust), out_shape=(s...]
where the time goes in v3:
time: 89.4 us; the launch traced here: 89.3 us
  Pallas kernels  86.2 us (96%)
  local copies, waits for them, and re-layouts  2.41 us (3%)
    pallas_call x2, Pallas kernels, local(): pl.pallas_call(packed(reduce_kernel, step, ny, nc), out_shape=(sd((NZ, co...  23.5 us
    pallas_call x1, Pallas kernels, local(): pl.pallas_call(functools.partial(gather_kernel, ny), out_shape=(sd((NZ, c...  21.7 us
    pallas_call x2, Pallas kernels, local(): pl.pallas_call(packed(step_kernel, step, ny), out_shape=outs, in_specs=[V...  17.6 us
    pallas_call x1, Pallas kernels, local(): pl.pallas_call(packed(reduce_kernel, step, ny, nc), out_shape=(sd((nf, 1,...  14.4 us
    pallas_call x1, Pallas kernels, local(): pl.pallas_call(packed(step_kernel, step, ny), out_shape=outs + (sd((ny, n...  9.06 us
    unnamed x4, local copies, waits for them, and re-layouts  1.89 us

profile of v3, /device:TPU:1, one launch (start us, length us, event | category | flops | bytes accessed | tf_op | source)
XLA Modules:
  0.0 89.3 jit_solution(2813767015884301039)
XLA Ops:
  0.6 21.7 %gather.1 = (bf16[8,512,128]{2,1,0:T(8,128)(2,1)S(1)}, bf16[4,512,128]{2,1,0:T(8,128)(2,1)S(1)}, f32[4,8,512]{2,1,0:T(8,128)S(1)}, f32[8,512]{1,0:T(8,128)S(1)},...) custom-call(bf16[512,128]{1,0:T(8,128)(2,1)} %cust_hbm.1, s32[1,512]{1,0:T(1,128)} %bitcast.11, ...), custom_call_target="tpu_custom_call" | custom-call | tf_op jit(solution)/shard_map/gather/pallas_call | solution.py:409
  22.3 9.1 %step.3 = (f32[4,512]{1,0:T(4,128)S(1)}, f32[8,512]{1,0:T(8,128)S(1)}, f32[1,128]{1,0:T(1,128)S(1)}, f32[4,512]{1,0:T(4,128)S(1)}, bf16[2528,128]{1,0:T(8,128)(2...) custom-call(bf16[4,512,128]{2,1,0:T(8,128)(2,1)S(1)} %get-tuple-element.30.refs_0_, ...), custom_call_target="tpu_custom_call" | custom-call | tf_op jit(solution)/shard_map/step/pallas_call | solution.py:428
  31.4 13.8 %reduce.3 = (f32[8,512]{1,0:T(8,128)S(1)}, f32[4,512]{1,0:T(4,128)S(1)}) custom-call(f32[4,512]{1,0:T(4,128)S(1)} %get-tuple-element.39.refs_0_, f32[8,512]{1,0:T(8,128)S(1)} %get-tuple-element.40.refs_1_, f32[8,512]{1,0:T(8,128)S(1)} %get-tuple-element.33.refs_3_.refs_2_, f32[8,512]{1,0:T(8,128)S(1)} %get-tuple-element.34.refs_4_.refs_3_.refs_6_, ...), custom_call_target="tpu_custom_call" | custom-call | tf_op jit(solution)/shard_map/reduce/pallas_call | solution.py:442
  45.1 8.9 %step.4 = (f32[4,512]{1,0:T(4,128)S(1)}, f32[8,512]{1,0:T(8,128)S(1)}, f32[1,128]{1,0:T(1,128)S(1)}) custom-call(bf16[2528,128]{1,0:T(8,128)(2,1)S(1)} %get-tuple-element.36.refs_0_, f32[4,8,512]{2,1,0:T(8,128)S(1)} %get-tuple-element.31.refs_1_.refs_5_, bf16[8,128,512]{2,1,0:T(8,128)(2,1)S(1)} %get-tuple-element.37.refs_2_, ...), custom_call_target="tpu_custom_call" | custom-call | tf_op jit(solution)/shard_map/step/pallas_call | solution.py:434
  54.0 9.7 %reduce.4 = (f32[8,512]{1,0:T(8,128)S(1)}, f32[4,512]{1,0:T(4,128)S(1)}) custom-call(f32[4,512]{1,0:T(4,128)S(1)} %get-tuple-element.45.refs_0_, f32[8,512]{1,0:T(8,128)S(1)} %get-tuple-element.46.refs_1_, f32[8,512]{1,0:T(8,128)S(1)} %get-tuple-element.43.refs_5_.refs_2_, f32[8,512]{1,0:T(8,128)S(1)} %get-tuple-element.34.refs_4_.refs_3_.refs_6_, ...), custom_call_target="tpu_custom_call" | custom-call | tf_op jit(solution)/shard_map/reduce/pallas_call | solution.py:442
  63.7 8.7 %step.5 = (f32[4,512]{1,0:T(4,128)S(1)}, f32[8,512]{1,0:T(8,128)S(1)}, f32[1,128]{1,0:T(1,128)S(1)}) custom-call(bf16[2528,128]{1,0:T(8,128)(2,1)S(1)} %get-tuple-element.36.refs_0_, f32[4,8,512]{2,1,0:T(8,128)S(1)} %get-tuple-element.31.refs_1_.refs_5_, bf16[8,128,512]{2,1,0:T(8,128)(2,1)S(1)} %get-tuple-element.37.refs_2_, ...), custom_call_target="tpu_custom_call" | custom-call | tf_op jit(solution)/shard_map/step/pallas_call | solution.py:434
  72.4 0.0 copy-start
  72.4 0.7 copy-done
  73.1 14.4 %reduce.5 = (f32[32,1,512]{2,1,0:T(1,128)S(1)}, f32[1,512]{1,0:T(1,128)S(1)}, f32[1,128]{1,0:T(1,128)S(1)}) custom-call(f32[4,512]{1,0:T(4,128)S(1)} %get-tuple-element.50.refs_0_, f32[8,512]{1,0:T(8,128)S(1)} %get-tuple-element.51.refs_1_, f32[8,512]{1,0:T(8,128)S(1)} %get-tuple-element.48.refs_5_.refs_2_, ...), custom_call_target="tpu_custom_call" | custom-call | tf_op jit(solution)/shard_map/reduce/pallas_call | solution.py:449
  87.6 0.5 slice_bitcast_fusion
  88.1 0.6 copy.13
  88.7 0.6 copy.14
Async XLA Ops:
  72.4 0.7 copy-start

commit v4 on v3

--- a/solution.py
+++ b/solution.py
@@ -84,8 +84,8 @@
 
 
 def gather_kernel(ny, cust_hbm, open_hbm, fac_hbm, cap_hbm, mu_hbm, fixed_hbm, demand_hbm, cover_hbm,
-                  all_ref, facs_ref, infos_ref, wt_ref, lam_ref, ext_ref, shut_ref,
-                  open_ref, fac_ref, cap_ref, mu_ref, fixed_ref, demand_ref, cover_ref, sz, rz, sy, ry, loc):
+                  facs_ref, infos_ref, wt_ref, lam_ref, ext_ref, shut_ref, flags_ref, turned_ref, hq_ref,
+                  all_ref, open_ref, fac_ref, cap_ref, mu_ref, fixed_ref, demand_ref, cover_ref, sz, rz, sy, ry, loc):
     y, z, c = spots()
     nz, cols = wt_ref.shape
     hops = NZ // 2
@@ -133,10 +133,20 @@
         shut = jnp.maximum(0.0, shut - 0.1 / (k + 1))
     ext_ref[...] = ext
     shut_ref[...] = shut
+    flags_ref[...] = open_ref[...]
     side = []
     for k, peer in enumerate(yp):
         side.append(remote(infos_ref.at[y], infos_ref.at[y], sy.at[k, 0], ry.at[k, 0], peer))
         side.append(remote(facs_ref.at[y], facs_ref.at[y], sy.at[k, 1], ry.at[k, 1], peer))
+    width = fac_ref.shape[1]
+    eye = (lax.broadcasted_iota(jnp.int32, (width, width), 0) == lax.broadcasted_iota(jnp.int32, (width, width), 1)).astype(F32).astype(BF16)
+
+    def turn(k):
+        turned = nt(eye, all_ref[k])
+        turned_ref[k] = turned.astype(BF16)
+        hq_ref[pl.ds(k, 1), :] = 0.5 * jnp.sum(turned * turned, axis=0, keepdims=True)
+
+    turn(z)
     for s in range(hops):
         for j in range(CHUNKS):
             for d in range(2):
@@ -144,6 +154,9 @@
                     ring[d, s, j].wait_recv()
                     if valid(d, s + 1, j):
                         ring[d, s + 1, j] = move(d, s + 1, j)
+        turn(lax.rem(z + s + 1, NZ))
+        if s < hops - 1:
+            turn(lax.rem(z + NZ - s - 1, NZ))
     for cpy in ring.values():
         cpy.wait_send()
     for cpy in side:
@@ -153,8 +166,8 @@
 def step_kernel(step, ny, refs):
     first = step == 0
     if first:
-        (facs_ref, infos_ref, cust_ref, lam_ref, wt_ref, ext_ref,
-         load_ref, cover_ref, tot_ref, mu_out_ref, coords_ref, turned_ref, hq_ref,
+        (facs_ref, infos_ref, turned_ref, hq_ref, lam_ref, wt_ref, ext_ref,
+         load_ref, cover_ref, tot_ref, mu_out_ref, coords_ref,
          a_ref, w_ref, y_ref, acc_ref, cov_ref, soft_ref, dw_ref, z_ref) = refs
     else:
         (coords_ref, infos_ref, turned_ref, hq_ref, mu_ref, lam_ref, wt_ref, ext_ref,
@@ -166,15 +179,7 @@
     total = nz * cols
     tiles = total // BLOCK
     me_y, me_z, c = spots()
-    if first:
-        eye = (lax.broadcasted_iota(jnp.int32, (width, width), 0) == lax.broadcasted_iota(jnp.int32, (width, width), 1)).astype(F32).astype(BF16)
-        for r in range(nz):
-            turned = nt(eye, cust_ref[r])
-            w_ref[r, 0:width, :] = turned.astype(BF16)
-            turned_ref[r] = turned.astype(BF16)
-            hq_ref[r:r + 1, :] = 0.5 * jnp.sum(turned * turned, axis=0, keepdims=True)
-    else:
-        w_ref[:, 0:width, :] = turned_ref[...]
+    w_ref[:, 0:width, :] = turned_ref[...]
     wt = wt_ref[...]
     lam = lam_ref[...]
     a1, a2, a3 = split3(64.0 * lam - hq_ref[...])
@@ -313,7 +318,7 @@
     gotz[z] = cover_ref[...]
     gotc[c] = load_ref[...]
     for cpy in cs:
-        cpy.wait()
+        cpy.wait_recv()
     total = gotc[0]
     for k in range(1, nc):
         total = total + gotc[k]
@@ -323,7 +328,7 @@
     if last:
         gott[z] = tot_ref[...]
         for cpy in ts:
-            cpy.wait()
+            cpy.wait_recv()
         total = gott[0]
         for k in range(1, NZ):
             total = total + gott[k]
@@ -331,7 +336,7 @@
         gotp[y * nc + c] = total
         ps = [remote(midt, gotp.at[y * nc + c], sp.at[d], rp.at[d], peer) for d, peer in enumerate(plane)]
     for cpy in zs:
-        cpy.wait()
+        cpy.wait_recv()
     cover = gotz[0]
     for k in range(1, NZ):
         cover = cover + gotz[k]
@@ -369,6 +374,21 @@
         bound_ref[...] = total / (NZ * ny * nc * lam_ref.shape[1])
         for cpy in ls:
             cpy.wait()
+        for cpy in ts:
+            cpy.wait_send()
+    for cpy in zs + cs:
+        cpy.wait_send()
+
+
+def finish_kernel(lam_ref, cap_ref, bound_ref, lam_out, cap_out, bound_out, sems):
+    copies = [pltpu.make_async_copy(lam_ref, lam_out, sems.at[0]), pltpu.make_async_copy(cap_ref, cap_out, sems.at[1])]
+    for cpy in copies:
+        cpy.start()
+    lane = lax.broadcasted_iota(jnp.int32, (1, 128), 1)
+    for k in range(ITERS):
+        bound_out[k] = jnp.sum(jnp.where(lane == k, bound_ref[...], 0.0))
+    for cpy in copies:
+        cpy.wait()
 
 
 def params(cid=None, mib=24):
@@ -406,12 +426,13 @@
     scr = pltpu.VMEM
     open_row = open_flags.reshape(1, n)
     hops = NZ // 2
-    cust, facs, infos, wt, lam, ext, shut = pl.pallas_call(
+    facs, infos, wt, lam, ext, shut, flags, turned, hq = pl.pallas_call(
         functools.partial(gather_kernel, ny),
-        out_shape=(sd((NZ, cols, width), BF16), sd((ny, n, width), BF16), sd((ny, 8, n), F32),
-                   sd((NZ, cols), F32), sd((NZ, cols), F32), sd((1, 128), F32), sd((1, n), F32)),
-        in_specs=[HBM] * 8, out_specs=(VMEM,) * 7,
-        scratch_shapes=[scr((1, n), jnp.int32), scr((n, width), BF16), scr((1, n), F32), scr((1, n), F32), scr((1, n), F32),
+        out_shape=(sd((ny, n, width), BF16), sd((ny, 8, n), F32),
+                   sd((NZ, cols), F32), sd((NZ, cols), F32), sd((1, 128), F32), sd((1, n), F32), sd((1, n), jnp.int32),
+                   sd((NZ, width, cols), BF16), sd((NZ, cols), F32)),
+        in_specs=[HBM] * 8, out_specs=(VMEM,) * 9,
+        scratch_shapes=[scr((NZ, cols, width), BF16), scr((1, n), jnp.int32), scr((n, width), BF16), scr((1, n), F32), scr((1, n), F32), scr((1, n), F32),
                         scr((1, NZ * cols), jnp.int32), scr((1, NZ * cols), F32),
                         dma((2, hops, CHUNKS)), dma((2, hops, CHUNKS)), dma((ny - 1, 2)), dma((ny - 1, 2)), dma((8,))],
         compiler_params=params(0), name="gather",
@@ -425,11 +446,11 @@
         last = step == ITERS - 1
         outs = (sd((ny, n), F32), sd((NZ, cols), F32), sd((1, 128), F32))
         if step == 0:
-            load, cover, tot, mu, coords, turned, hq = pl.pallas_call(
+            load, cover, tot, mu, coords = pl.pallas_call(
                 packed(step_kernel, step, ny),
-                out_shape=outs + (sd((ny, n), F32), sd((rows, width), BF16), sd((NZ, width, cols), BF16), sd((NZ, cols), F32)),
-                in_specs=[VMEM] * 6, out_specs=(VMEM,) * 7, scratch_shapes=work, compiler_params=params(), name="step",
-            )(facs, infos, cust, lam, wt, tot)
+                out_shape=outs + (sd((ny, n), F32), sd((rows, width), BF16)),
+                in_specs=[VMEM] * 7, out_specs=(VMEM,) * 5, scratch_shapes=work, compiler_params=params(), name="step",
+            )(facs, infos, turned, hq, lam, wt, tot)
         else:
             load, cover, tot = pl.pallas_call(
                 packed(step_kernel, step, ny),
@@ -453,8 +474,13 @@
                     scr((NZ, 1, 128), F32), scr((plane, 1, 128), F32), scr((1, 128), F32), scr((NZ, 1, cols), F32),
                     dma((NZ - 1,)), dma((NZ - 1,)), dma((plane - 1,)), dma((plane - 1,)), dma((ny - 1,)), dma((ny - 1,))],
                 compiler_params=params(1 + step), name="reduce",
-            )(load, cover, lam, wt, mu, infos, tot, open_row, shut)
-    return lam_all.reshape(nf * cols), cap_final.reshape(n), bounds[0, :ITERS]
+            )(load, cover, lam, wt, mu, infos, tot, flags, shut)
+    lam_all, cap_final, bounds = pl.pallas_call(
+        finish_kernel, out_shape=(sd((nf, 1, cols), F32), sd((1, n), F32), sd((ITERS,), F32)),
+        in_specs=[VMEM] * 3, out_specs=(HBM, HBM, pl.BlockSpec(memory_space=pltpu.SMEM)), scratch_shapes=[dma((2,))],
+        compiler_params=params(), name="finish",
+    )(lam_all, cap_final, bounds)
+    return lam_all.reshape(nf * cols), cap_final.reshape(n), bounds
 
 
 def solution(mesh):

time: 89.4 us -> 89.2 us (level)
  Pallas kernels: 86.2 us -> 88.9 us
  local copies, waits for them, and re-layouts: 2.41 us -> 0 us
    pallas_call x2, Pallas kernels: 17.6 us -> 19.6 us  [local(): pl.pallas_call(packed(step_kernel, step, ny), out_shape=outs, in_specs=[V...]
    unnamed x4 -> x0, local copies, waits for them, and re-layouts: 1.89 us -> none
    pallas_call x1 -> x2, Pallas kernels: 21.7 us -> 23.1 us  [the longest x1 21.9 us: local(): pl.pallas_call(functools.partial(gather_kernel, ny), out_shape=(sd((ny, n...]
    pallas_call x2, Pallas kernels: 23.5 us -> 22.2 us  [local(): pl.pallas_call(packed(reduce_kernel, step, ny, nc), out_shape=(sd((NZ, co...]
where the time goes in v4:
time: 89.2 us; the launch traced here: 89.7 us
  Pallas kernels  88.9 us (100%)
    pallas_call x2, Pallas kernels, local(): pl.pallas_call(packed(reduce_kernel, step, ny, nc), out_shape=(sd((NZ, co...  22.2 us
    pallas_call x1, Pallas kernels, local(): pl.pallas_call(functools.partial(gather_kernel, ny), out_shape=(sd((ny, n...  21.9 us
    pallas_call x2, Pallas kernels, local(): pl.pallas_call(packed(step_kernel, step, ny), out_shape=outs, in_specs=[V...  19.6 us
    pallas_call x1, Pallas kernels, local(): pl.pallas_call(packed(reduce_kernel, step, ny, nc), out_shape=(sd((nf, 1,...  14.3 us
    pallas_call x1, Pallas kernels, local(): pl.pallas_call(packed(step_kernel, step, ny), out_shape=outs + (sd((ny, n...  9.81 us

profile of v4, /device:TPU:1, one launch (start us, length us, event | category | flops | bytes accessed | tf_op | source)
XLA Modules:
  0.0 89.7 jit_solution(18000241916081842213)
XLA Ops:
  0.6 21.9 %gather.1 = (bf16[4,512,128]{2,1,0:T(8,128)(2,1)S(1)}, f32[4,8,512]{2,1,0:T(8,128)S(1)}, f32[8,512]{1,0:T(8,128)S(1)}, f32[8,512]{1,0:T(8,128)S(1)}, f32[1,128]{...) custom-call(bf16[512,128]{1,0:T(8,128)(2,1)} %cust_hbm.1, ...), custom_call_target="tpu_custom_call" | custom-call | tf_op jit(solution)/shard_map/gather/pallas_call | solution.py:429
  22.5 9.8 %step.3 = (f32[4,512]{1,0:T(4,128)S(1)}, f32[8,512]{1,0:T(8,128)S(1)}, f32[1,128]{1,0:T(1,128)S(1)}, f32[4,512]{1,0:T(4,128)S(1)}, bf16[2528,128]{1,0:T(8,128)(2,1)S(1)}) custom-call(bf16[4,512,128]{2,1,0:T(8,128)(2,1)S(1)} %get-tuple-element.33.refs_0_, f32[4,8,512]{2,1,0:T(8,128)S(1)} %get-tuple-element.34.refs_1_.refs_5_, ...), custom_call_target="tpu_custom_call" | custom-call | tf_op jit(solution)/shard_map/step/pallas_call | solution.py:449
  32.3 12.8 %reduce.3 = (f32[8,512]{1,0:T(8,128)S(1)}, f32[4,512]{1,0:T(4,128)S(1)}) custom-call(f32[4,512]{1,0:T(4,128)S(1)} %get-tuple-element.41.refs_0_, f32[8,512]{1,0:T(8,128)S(1)} %get-tuple-element.42.refs_1_, f32[8,512]{1,0:T(8,128)S(1)} %get-tuple-element.37.refs_4_.refs_2_, f32[8,512]{1,0:T(8,128)S(1)} %get-tuple-element.38.refs_5_.refs_3_.refs_6_, ...), custom_call_target="tpu_custom_call" | custom-call | tf_op jit(solution)/shard_map/reduce/pallas_call | solution.py:463
  45.1 9.9 %step.4 = (f32[4,512]{1,0:T(4,128)S(1)}, f32[8,512]{1,0:T(8,128)S(1)}, f32[1,128]{1,0:T(1,128)S(1)}) custom-call(bf16[2528,128]{1,0:T(8,128)(2,1)S(1)} %get-tuple-element.40.refs_0_, f32[4,8,512]{2,1,0:T(8,128)S(1)} %get-tuple-element.34.refs_1_.refs_5_, bf16[8,128,512]{2,1,0:T(8,128)(2,1)S(1)} %get-tuple-element.35.refs_2_, ...), custom_call_target="tpu_custom_call" | custom-call | tf_op jit(solution)/shard_map/step/pallas_call | solution.py:455
  55.0 9.5 %reduce.4 = (f32[8,512]{1,0:T(8,128)S(1)}, f32[4,512]{1,0:T(4,128)S(1)}) custom-call(f32[4,512]{1,0:T(4,128)S(1)} %get-tuple-element.47.refs_0_, f32[8,512]{1,0:T(8,128)S(1)} %get-tuple-element.48.refs_1_, f32[8,512]{1,0:T(8,128)S(1)} %get-tuple-element.45.refs_5_.refs_2_, f32[8,512]{1,0:T(8,128)S(1)} %get-tuple-element.38.refs_5_.refs_3_.refs_6_, ...), custom_call_target="tpu_custom_call" | custom-call | tf_op jit(solution)/shard_map/reduce/pallas_call | solution.py:463
  64.4 9.7 %step.5 = (f32[4,512]{1,0:T(4,128)S(1)}, f32[8,512]{1,0:T(8,128)S(1)}, f32[1,128]{1,0:T(1,128)S(1)}) custom-call(bf16[2528,128]{1,0:T(8,128)(2,1)S(1)} %get-tuple-element.40.refs_0_, f32[4,8,512]{2,1,0:T(8,128)S(1)} %get-tuple-element.34.refs_1_.refs_5_, bf16[8,128,512]{2,1,0:T(8,128)(2,1)S(1)} %get-tuple-element.35.refs_2_, ...), custom_call_target="tpu_custom_call" | custom-call | tf_op jit(solution)/shard_map/step/pallas_call | solution.py:455
  74.1 14.3 %reduce.5 = (f32[32,1,512]{2,1,0:T(1,128)S(1)}, f32[1,512]{1,0:T(1,128)S(1)}, f32[1,128]{1,0:T(1,128)S(1)}) custom-call(f32[4,512]{1,0:T(4,128)S(1)} %get-tuple-element.52.refs_0_, f32[8,512]{1,0:T(8,128)S(1)} %get-tuple-element.53.refs_1_, f32[8,512]{1,0:T(8,128)S(1)} %get-tuple-element.50.refs_5_.refs_2_, ...), custom_call_target="tpu_custom_call" | custom-call | tf_op jit(solution)/shard_map/reduce/pallas_call | solution.py:470
  88.4 1.2 %finish.1 = (f32[32,1,512]{2,1,0:T(1,128)}, f32[1,512]{1,0:T(1,128)}, f32[3]{0:T(128)}) custom-call(f32[32,1,512]{2,1,0:T(1,128)S(1)} %get-tuple-element.57.lam_ref, f32[1,512]{1,0:T(1,128)S(1)} %get-tuple-element.58.cap_ref, f32[1,128]{1,0:T(1,128)S(1)} %get-tuple-element.59.bound_ref), custom_call_target="tpu_custom_call" | custom-call | tf_op jit(solution)/shard_map/finish/pallas_call | solution.py:478

commit v5 on v4

--- a/solution.py
+++ b/solution.py
@@ -13,6 +13,7 @@
 TAU = 0.1
 ALIGN = 16
 ROWS = 160
+HEAD = 160
 BLOCK = 512
 CHUNKS = 8
 NZ = 8
@@ -53,11 +54,15 @@
     return f // NZ, lax.rem(f, NZ), c
 
 
-def sync(peers):
+def greet(peers):
     barrier = pltpu.get_barrier_semaphore()
     for peer in peers:
         pl.semaphore_signal(barrier, inc=1, device_id=peer, device_id_type=MESH)
-    pl.semaphore_wait(barrier, len(peers))
+
+
+def sync(peers):
+    greet(peers)
+    pl.semaphore_wait(pltpu.get_barrier_semaphore(), len(peers))
 
 
 def remote(src, dst, send, recv, peer):
@@ -167,12 +172,12 @@
     first = step == 0
     if first:
         (facs_ref, infos_ref, turned_ref, hq_ref, lam_ref, wt_ref, ext_ref,
-         load_ref, cover_ref, tot_ref, mu_out_ref, coords_ref,
-         a_ref, w_ref, y_ref, acc_ref, cov_ref, soft_ref, dw_ref, z_ref) = refs
+         load_ref, cover_ref, tot_ref, w_ref, head_ref, mu_out_ref, coords_ref,
+         a_ref, y_ref, acc_ref, cov_ref, soft_ref, dw_ref, z_ref) = refs
     else:
         (coords_ref, infos_ref, turned_ref, hq_ref, mu_ref, lam_ref, wt_ref, ext_ref,
-         load_ref, cover_ref, tot_ref,
-         a_ref, w_ref, y_ref, acc_ref, cov_ref, soft_ref, dw_ref, z_ref) = refs
+         load_ref, cover_ref, tot_ref, w_ref, head_ref,
+         a_ref, y_ref, acc_ref, cov_ref, soft_ref, dw_ref, z_ref) = refs
     n = infos_ref.shape[2]
     nz, cols = lam_ref.shape
     width = coords_ref.shape[1]
@@ -220,24 +225,27 @@
             a_ref[pl.ds(off, n), 0:width] = facs_ref[s]
         a_ref[pl.ds(off, n), width:2 * width] = side
         off = off + ((count + ALIGN - 1) // ALIGN) * ALIGN
+        if s == 0:
+            off = jnp.maximum(off, HEAD)
     tail = pl.multiple_of(off, ALIGN)
     if first:
         a_ref[pl.ds(tail, ROWS), 0:width] = jnp.zeros((ROWS, width), BF16)
     a_ref[pl.ds(tail, ROWS), width:2 * width] = pad
     if first:
         coords_ref[...] = a_ref[:, 0:width]
-    n_blocks = (off + ROWS - 1) // ROWS
+    head_ref[...] = a_ref[0:HEAD, :]
+    n_blocks = (off - HEAD + ROWS - 1) // ROWS
     scale = math.log2(math.e) / 6.4
 
     def dot(base, t, out):
         out[t] = jnp.dot(a_ref[pl.ds(base, ROWS), :], w_ref[t], preferred_element_type=F32)
 
     def phase(i, cur, nxt, opening=False):
-        base = pl.multiple_of(i * ROWS, ROWS)
+        base = pl.multiple_of(HEAD + i * ROWS, 32)
         for t in range(tiles):
             if opening and t + 1 < tiles:
-                dot(0, t + 1, cur)
-            dot(pl.multiple_of(base + ROWS, ROWS), t, nxt)
+                dot(HEAD, t + 1, cur)
+            dot(pl.multiple_of(base + ROWS, 32), t, nxt)
             spans = [slice(t * BLOCK + q * 128, t * BLOCK + (q + 1) * 128) for q in range(BLOCK // 128)]
             covs = [cov_ref[:, at] for at in spans]
             softs = [soft_ref[:, at] for at in spans]
@@ -267,7 +275,8 @@
         pl.when(2 * i + 2 < n_blocks)(lambda: phase(2 * i + 2, y_ref, z_ref))
         return 0
 
-    dot(0, 0, y_ref)
+    dot(HEAD, 0, y_ref)
+    acc_ref[0:HEAD, :] = jnp.zeros((HEAD, 128), F32)
     phase(jnp.int32(0), y_ref, z_ref, True)
     lax.fori_loop(0, n_blocks // 2, body, 0)
     ones = jnp.ones((16, 128), BF16)
@@ -279,7 +288,7 @@
     soft = 0.0
     for r in range(nz):
         at = slice(r * cols, (r + 1) * cols)
-        cover_ref[r:r + 1, :] = jnp.sum(cov_ref[:, at], axis=0, keepdims=True) / wt[r:r + 1]
+        cover_ref[r:r + 1, :] = jnp.sum(cov_ref[:, at], axis=0, keepdims=True)
         soft = soft + soft_ref[:, at] * wt[r:r + 1]
     mu_all = mu_out_ref if first else mu_ref
     caps = infos_ref[me_y, 3:4, :]
@@ -290,6 +299,39 @@
     tot_ref[...] = ext_ref[...] + jnp.where(spot, here, 0.0)
 
 
+def head_rows(wt_ref, w_ref, head_ref, hy, hacc, hcov):
+    tiles = w_ref.shape[0]
+    scale = math.log2(math.e) / 6.4
+    for t in range(tiles):
+        hy[t] = jnp.dot(head_ref[...], w_ref[t], preferred_element_type=F32)
+    hacc[...] = jnp.zeros_like(hacc)
+
+    def body(t, soft):
+        covs = [jnp.zeros((16, 128), F32)] * (BLOCK // 128)
+        softs = [jnp.zeros((8, 128), F32)] * (BLOCK // 128)
+        weights = wt_ref[pl.ds(t, 1), :]
+        for r in range(0, HEAD, 32):
+            loads = [hacc[r:r + 16, :], hacc[r + 16:r + 32, :]]
+            for q in range(BLOCK // 128):
+                at = slice(q * 128, (q + 1) * 128)
+                es = [jnp.exp2(hy[t, r + 16 * s:r + 16 * s + 16, at] * scale) for s in range(2)]
+                us = [1.0 + e for e in es]
+                p = us[0] * us[1]
+                inv = weights[:, at] / p
+                xs = [es[0] * (us[1] * inv), es[1] * (us[0] * inv)]
+                loads = [a + x for a, x in zip(loads, xs)]
+                covs[q] = covs[q] + (xs[0] + xs[1])
+                softs[q] = softs[q] + jnp.log(p[0:8] * p[8:16])
+            hacc[r:r + 16, :] = loads[0]
+            hacc[r + 16:r + 32, :] = loads[1]
+        hcov[pl.ds(t, 1), :] = jnp.concatenate([jnp.sum(v, axis=0, keepdims=True) for v in covs], axis=1)
+        for q in range(BLOCK // 128):
+            soft = soft + softs[q] * weights[:, q * 128:(q + 1) * 128]
+        return soft
+
+    return jnp.sum(lax.fori_loop(0, tiles, body, jnp.zeros((8, 128), F32)))
+
+
 def far(n):
     return sorted(range(1, n), key=lambda d: -min(d, n - d))
 
@@ -297,12 +339,12 @@
 def reduce_kernel(step, ny, nc, refs):
     last = step == ITERS - 1
     if last:
-        (load_ref, cover_ref, lam_ref, wt_ref, mu_ref, infos_ref, tot_ref, open_ref, shut_ref,
-         lam_out_ref, cap_out_ref, bound_ref, mu_out_ref,
+        (load_ref, cover_ref, lam_ref, wt_ref, mu_ref, infos_ref, tot_ref, w_ref, head_ref, open_ref, shut_ref,
+         lam_out_ref, cap_out_ref, bound_ref, mu_out_ref, tot_out_ref, hy, hacc, hcov, hload,
          gotz, gotc, goty, mid, sz, rz, sc, rc, sy, ry, gott, gotp, midt, own, st, rt, sp, rp, sl, rl) = refs
     else:
-        (load_ref, cover_ref, lam_ref, wt_ref, mu_ref, infos_ref,
-         lam_out_ref, mu_out_ref,
+        (load_ref, cover_ref, lam_ref, wt_ref, mu_ref, infos_ref, tot_ref, w_ref, head_ref,
+         lam_out_ref, mu_out_ref, tot_out_ref, hy, hacc, hcov, hload,
          gotz, gotc, goty, mid, sz, rz, sc, rc, sy, ry) = refs
     size = 0.1 / (step + 1)
     y, z, c = spots()
@@ -310,13 +352,21 @@
     yp = [(lax.rem(y + d, ny) * NZ + z, c) for d in far(ny)]
     cp = [(y * NZ + z, lax.rem(c + d, nc)) for d in far(nc)]
     plane = [(lax.rem(y + e, ny) * NZ + z, lax.rem(c + d, nc)) for e in far(ny) + [0] for d in far(nc) + [0] if e + d > 0]
-    sync(zp + (plane if last else yp + cp))
+    peers = zp + (plane if last else yp + cp)
+    greet(peers)
+    tot_out_ref[...] = tot_ref[...] - jnp.where(lax.broadcasted_iota(jnp.int32, (1, 128), 1) == step, TAU * head_rows(wt_ref, w_ref, head_ref, hy, hacc, hcov), 0.0)
+    gotz[z] = (cover_ref[...] + hcov[...]) / wt_ref[...]
+    ones = jnp.ones((16, 128), BF16)
+    hload[...] = load_ref[...]
+    for b in range(2):
+        at = slice(b * 128, (b + 1) * 128)
+        hload[0:1, at] = load_ref[0:1, at] + sum(nt(ones, p)[0:1] for p in split3(hacc[at, :])[:2])
+    gotc[c] = hload[...]
+    pl.semaphore_wait(pltpu.get_barrier_semaphore(), len(peers))
     if last:
-        ts = [remote(tot_ref, gott.at[z], st.at[d], rt.at[d], peer) for d, peer in enumerate(zp)]
-    zs = [remote(cover_ref, gotz.at[z], sz.at[d], rz.at[d], peer) for d, peer in enumerate(zp)]
-    cs = [remote(load_ref, gotc.at[c], sc.at[d], rc.at[d], peer) for d, peer in enumerate(cp)]
-    gotz[z] = cover_ref[...]
-    gotc[c] = load_ref[...]
+        ts = [remote(tot_out_ref, gott.at[z], st.at[d], rt.at[d], peer) for d, peer in enumerate(zp)]
+    zs = [remote(gotz.at[z], gotz.at[z], sz.at[d], rz.at[d], peer) for d, peer in enumerate(zp)]
+    cs = [remote(gotc.at[c], gotc.at[c], sc.at[d], rc.at[d], peer) for d, peer in enumerate(cp)]
     for cpy in cs:
         cpy.wait_recv()
     total = gotc[0]
@@ -326,7 +376,7 @@
     goty[y] = total
     ys = [remote(mid, goty.at[y], sy.at[d], ry.at[d], peer) for d, peer in enumerate(yp)]
     if last:
-        gott[z] = tot_ref[...]
+        gott[z] = tot_out_ref[...]
         for cpy in ts:
             cpy.wait_recv()
         total = gott[0]
@@ -403,11 +453,10 @@
 
 def work_of(ny, n, cols, width):
     scr = pltpu.VMEM
-    rows = ny * n + 3 * ROWS
+    rows = ny * n + HEAD + 3 * ROWS
     total = NZ * cols
     return rows, [
         scr((rows, 2 * width), BF16),
-        scr((total // BLOCK, 2 * width, BLOCK), BF16),
         scr((total // BLOCK, ROWS, BLOCK), F32),
         scr((rows, 128), F32),
         scr((8, total), F32),
@@ -444,37 +493,38 @@
     mu = None
     for step in range(ITERS):
         last = step == ITERS - 1
-        outs = (sd((ny, n), F32), sd((NZ, cols), F32), sd((1, 128), F32))
+        outs = (sd((ny, n), F32), sd((NZ, cols), F32), sd((1, 128), F32), sd((NZ, 2 * width, cols), BF16), sd((HEAD, 2 * width), BF16))
         if step == 0:
-            load, cover, tot, mu, coords = pl.pallas_call(
+            load, cover, tot, w, head, mu, coords = pl.pallas_call(
                 packed(step_kernel, step, ny),
                 out_shape=outs + (sd((ny, n), F32), sd((rows, width), BF16)),
-                in_specs=[VMEM] * 7, out_specs=(VMEM,) * 5, scratch_shapes=work, compiler_params=params(), name="step",
+                in_specs=[VMEM] * 7, out_specs=(VMEM,) * 7, scratch_shapes=work, compiler_params=params(), name="step",
             )(facs, infos, turned, hq, lam, wt, tot)
         else:
-            load, cover, tot = pl.pallas_call(
+            load, cover, tot, w, head = pl.pallas_call(
                 packed(step_kernel, step, ny),
-                out_shape=outs, in_specs=[VMEM] * 8, out_specs=(VMEM,) * 3, scratch_shapes=work,
+                out_shape=outs, in_specs=[VMEM] * 8, out_specs=(VMEM,) * 5, scratch_shapes=work,
                 compiler_params=params(), name="step",
             )(coords, infos, turned, hq, mu, lam, wt, tot)
+        front = [scr((NZ, HEAD, cols), F32), scr((256, 128), F32), scr((NZ, cols), F32), scr((ny, n), F32)]
         scratch = [scr((NZ, NZ, cols), F32), scr((nc, ny, n), F32), scr((ny, ny, n), F32), scr((ny, n), F32),
                    dma((NZ - 1,)), dma((NZ - 1,)), dma((nc - 1,)), dma((nc - 1,)), dma((ny - 1,)), dma((ny - 1,))]
         if not last:
-            lam, mu = pl.pallas_call(
+            lam, mu, tot = pl.pallas_call(
                 packed(reduce_kernel, step, ny, nc),
-                out_shape=(sd((NZ, cols), F32), sd((ny, n), F32)), in_specs=[VMEM] * 6, out_specs=(VMEM,) * 2,
-                scratch_shapes=scratch, compiler_params=params(1 + step), name="reduce",
-            )(load, cover, lam, wt, mu, infos)
+                out_shape=(sd((NZ, cols), F32), sd((ny, n), F32), sd((1, 128), F32)), in_specs=[VMEM] * 9, out_specs=(VMEM,) * 3,
+                scratch_shapes=front + scratch, compiler_params=params(1 + step), name="reduce",
+            )(load, cover, lam, wt, mu, infos, tot, w, head)
         else:
             plane = ny * nc
             lam_all, cap_final, bounds = pl.pallas_call(
                 packed(reduce_kernel, step, ny, nc),
-                out_shape=(sd((nf, 1, cols), F32), sd((1, n), F32), sd((1, 128), F32)), in_specs=[VMEM] * 9, out_specs=(VMEM,) * 3,
-                scratch_shapes=[scr((ny, n), F32)] + scratch + [
+                out_shape=(sd((nf, 1, cols), F32), sd((1, n), F32), sd((1, 128), F32)), in_specs=[VMEM] * 11, out_specs=(VMEM,) * 3,
+                scratch_shapes=[scr((ny, n), F32), scr((1, 128), F32)] + front + scratch + [
                     scr((NZ, 1, 128), F32), scr((plane, 1, 128), F32), scr((1, 128), F32), scr((NZ, 1, cols), F32),
                     dma((NZ - 1,)), dma((NZ - 1,)), dma((plane - 1,)), dma((plane - 1,)), dma((ny - 1,)), dma((ny - 1,))],
                 compiler_params=params(1 + step), name="reduce",
-            )(load, cover, lam, wt, mu, infos, tot, flags, shut)
+            )(load, cover, lam, wt, mu, infos, tot, w, head, flags, shut)
     lam_all, cap_final, bounds = pl.pallas_call(
         finish_kernel, out_shape=(sd((nf, 1, cols), F32), sd((1, n), F32), sd((ITERS,), F32)),
         in_specs=[VMEM] * 3, out_specs=(HBM, HBM, pl.BlockSpec(memory_space=pltpu.SMEM)), scratch_shapes=[dma((2,))],

time: 89.2 us -> 85.3 us (0.956)
  Pallas kernels: 88.9 us -> 84.4 us
    pallas_call x2, Pallas kernels: 19.6 us -> 15.4 us  [local(): pl.pallas_call(packed(step_kernel, step, ny), out_shape=outs, in_specs=[V...]
    pallas_call x1, Pallas kernels: 9.81 us -> 7.74 us  [local(): pl.pallas_call(packed(step_kernel, step, ny), out_shape=outs + (sd((ny, n...]
    pallas_call x2, Pallas kernels: 22.2 us -> 23.5 us  [local(): pl.pallas_call(packed(reduce_kernel, step, ny, nc), out_shape=(sd((NZ, co...]
where the time goes in v5:
time: 85.3 us
  Pallas kernels  84.4 us (99%)
    pallas_call x2, Pallas kernels, local(): pl.pallas_call(packed(reduce_kernel, step, ny, nc), out_shape=(sd((NZ, co...  23.5 us
    pallas_call x1, Pallas kernels, local(): pl.pallas_call(functools.partial(gather_kernel, ny), out_shape=(sd((ny, n...  21.9 us
    pallas_call x2, Pallas kernels, local(): pl.pallas_call(packed(step_kernel, step, ny), out_shape=outs, in_specs=[V...  15.4 us
    pallas_call x1, Pallas kernels, local(): pl.pallas_call(packed(reduce_kernel, step, ny, nc), out_shape=(sd((nf, 1,...  14.7 us
    pallas_call x1, Pallas kernels, local(): pl.pallas_call(packed(step_kernel, step, ny), out_shape=outs + (sd((ny, n...  7.74 us

profile of v5, /device:TPU:1, one launch (start us, length us, event | category | flops | bytes accessed | tf_op | source)
XLA Modules:
  0.0 85.3 jit_solution(5227845977377589984)
XLA Ops:
  0.6 21.9 %gather.1 = (bf16[4,512,128]{2,1,0:T(8,128)(2,1)S(1)}, f32[4,8,512]{2,1,0:T(8,128)S(1)}, f32[8,512]{1,0:T(8,128)S(1)}, f32[8,512]{1,0:T(8,128)S(1)}, f32[1,128]{...) custom-call(bf16[512,128]{1,0:T(8,128)(2,1)} %cust_hbm.1, ...), custom_call_target="tpu_custom_call" | custom-call | tf_op jit(solution)/shard_map/gather/pallas_call | solution.py:478
  22.5 7.7 %step.3 = (f32[4,512]{1,0:T(4,128)S(1)}, f32[8,512]{1,0:T(8,128)S(1)}, f32[1,128]{1,0:T(1,128)S(1)}, bf16[8,256,512]{2,1,0:T(8,128)(2,1)S(1)}, bf16[160,256]{1,0...) custom-call(bf16[4,512,128]{2,1,0:T(8,128)(2,1)S(1)} %get-tuple-element.41.refs_0_, ...), custom_call_target="tpu_custom_call" | custom-call | tf_op jit(solution)/shard_map/step/pallas_call | solution.py:498
  30.3 13.8 %reduce.3 = (f32[8,512]{1,0:T(8,128)S(1)}, f32[4,512]{1,0:T(4,128)S(1)}, f32[1,128]{1,0:T(1,128)S(1)}) custom-call(f32[4,512]{1,0:T(4,128)S(1)} %get-tuple-element.49.refs_0_, f32[8,512]{1,0:T(8,128)S(1)} %get-tuple-element.50.refs_1_, f32[8,512]{1,0:T(8,128)S(1)} %get-tuple-element.45.refs_4_.refs_2_, ...), custom_call_target="tpu_custom_call" | custom-call | tf_op jit(solution)/shard_map/reduce/pallas_call | solution.py:513
  44.1 7.8 %step.4 = (f32[4,512]{1,0:T(4,128)S(1)}, f32[8,512]{1,0:T(8,128)S(1)}, f32[1,128]{1,0:T(1,128)S(1)}, bf16[8,256,512]{2,1,0:T(8,128)(2,1)S(1)}, bf16[160,256]{1,0:T(8,128)(2,1)S(1)}) custom-call(bf16[2688,128]{1,0:T(8,128)(2,1)S(1)} %get-tuple-element.48.refs_0_, f32[4,8,512]{2,1,0:T(8,128)S(1)} %get-tuple-element.42.refs_1_.refs_5_, ...), custom_call_target="tpu_custom_call" | custom-call | tf_op jit(solution)/shard_map/step/pallas_call | solution.py:504
  51.9 9.7 %reduce.4 = (f32[8,512]{1,0:T(8,128)S(1)}, f32[4,512]{1,0:T(4,128)S(1)}, f32[1,128]{1,0:T(1,128)S(1)}) custom-call(f32[4,512]{1,0:T(4,128)S(1)} %get-tuple-element.58.refs_0_, f32[8,512]{1,0:T(8,128)S(1)} %get-tuple-element.59.refs_1_, f32[8,512]{1,0:T(8,128)S(1)} %get-tuple-element.56.refs_5_.refs_2_, ...), custom_call_target="tpu_custom_call" | custom-call | tf_op jit(solution)/shard_map/reduce/pallas_call | solution.py:513
  61.6 7.6 %step.5 = (f32[4,512]{1,0:T(4,128)S(1)}, f32[8,512]{1,0:T(8,128)S(1)}, f32[1,128]{1,0:T(1,128)S(1)}, bf16[8,256,512]{2,1,0:T(8,128)(2,1)S(1)}, bf16[160,256]{1,0:T(8,128)(2,1)S(1)}) custom-call(bf16[2688,128]{1,0:T(8,128)(2,1)S(1)} %get-tuple-element.48.refs_0_, f32[4,8,512]{2,1,0:T(8,128)S(1)} %get-tuple-element.42.refs_1_.refs_5_, ...), custom_call_target="tpu_custom_call" | custom-call | tf_op jit(solution)/shard_map/step/pallas_call | solution.py:504
  69.2 14.7 %reduce.5 = (f32[32,1,512]{2,1,0:T(1,128)S(1)}, f32[1,512]{1,0:T(1,128)S(1)}, f32[1,128]{1,0:T(1,128)S(1)}) custom-call(f32[4,512]{1,0:T(4,128)S(1)} %get-tuple-element.66.refs_0_, f32[8,512]{1,0:T(8,128)S(1)} %get-tuple-element.67.refs_1_, f32[8,512]{1,0:T(8,128)S(1)} %get-tuple-element.64.refs_5_.refs_2_, ...), custom_call_target="tpu_custom_call" | custom-call | tf_op jit(solution)/shard_map/reduce/pallas_call | solution.py:520
  83.9 1.2 %finish.1 = (f32[32,1,512]{2,1,0:T(1,128)}, f32[1,512]{1,0:T(1,128)}, f32[3]{0:T(128)}) custom-call(f32[32,1,512]{2,1,0:T(1,128)S(1)} %get-tuple-element.73.lam_ref, f32[1,512]{1,0:T(1,128)S(1)} %get-tuple-element.74.cap_ref, f32[1,128]{1,0:T(1,128)S(1)} %get-tuple-element.75.bound_ref), custom_call_target="tpu_custom_call" | custom-call | tf_op jit(solution)/shard_map/finish/pallas_call | solution.py:528

commit v6 on v5

--- a/solution.py
+++ b/solution.py
@@ -13,7 +13,7 @@
 TAU = 0.1
 ALIGN = 16
 ROWS = 160
-HEAD = 160
+HEAD = 80
 BLOCK = 512
 CHUNKS = 8
 NZ = 8
@@ -175,7 +175,7 @@
          load_ref, cover_ref, tot_ref, w_ref, head_ref, mu_out_ref, coords_ref,
          a_ref, y_ref, acc_ref, cov_ref, soft_ref, dw_ref, z_ref) = refs
     else:
-        (coords_ref, infos_ref, turned_ref, hq_ref, mu_ref, lam_ref, wt_ref, ext_ref,
+        (coords_ref, before_ref, infos_ref, turned_ref, hq_ref, mu_ref, lam_ref, wt_ref, ext_ref,
          load_ref, cover_ref, tot_ref, w_ref, head_ref,
          a_ref, y_ref, acc_ref, cov_ref, soft_ref, dw_ref, z_ref) = refs
     n = infos_ref.shape[2]
@@ -203,10 +203,11 @@
     pad = jnp.where(lane == 3, -30000.0, 0.0).astype(BF16)
     sel = (lax.broadcasted_iota(jnp.int32, (16, width), 0) == lax.broadcasted_iota(jnp.int32, (16, width), 1)).astype(F32).astype(BF16)
     offs = []
-    off = jnp.int32(0)
+    off = jnp.int32(HEAD)
     one_r = jnp.ones((3, n), F32)
     if not first:
         a_ref[:, 0:width] = coords_ref[...]
+        head_ref[:, 0:width] = before_ref[:, 0:width]
     for s in range(ny):
         valid = infos_ref[s, 0:1, :]
         if first:
@@ -222,18 +223,17 @@
         off = pl.multiple_of(off, ALIGN)
         offs.append(off)
         if first:
-            a_ref[pl.ds(off, n), 0:width] = facs_ref[s]
-        a_ref[pl.ds(off, n), width:2 * width] = side
-        off = off + ((count + ALIGN - 1) // ALIGN) * ALIGN
-        if s == 0:
-            off = jnp.maximum(off, HEAD)
+            a_ref[pl.ds(off, n - HEAD), 0:width] = facs_ref[s, HEAD:]
+            head_ref[s * HEAD:(s + 1) * HEAD, 0:width] = facs_ref[s, 0:HEAD]
+        a_ref[pl.ds(off, n - HEAD), width:2 * width] = side[HEAD:]
+        head_ref[s * HEAD:(s + 1) * HEAD, width:2 * width] = side[0:HEAD]
+        off = off + ((jnp.maximum(count - HEAD, 0) + ALIGN - 1) // ALIGN) * ALIGN
     tail = pl.multiple_of(off, ALIGN)
     if first:
         a_ref[pl.ds(tail, ROWS), 0:width] = jnp.zeros((ROWS, width), BF16)
     a_ref[pl.ds(tail, ROWS), width:2 * width] = pad
     if first:
         coords_ref[...] = a_ref[:, 0:width]
-    head_ref[...] = a_ref[0:HEAD, :]
     n_blocks = (off - HEAD + ROWS - 1) // ROWS
     scale = math.log2(math.e) / 6.4
 
@@ -241,11 +241,11 @@
         out[t] = jnp.dot(a_ref[pl.ds(base, ROWS), :], w_ref[t], preferred_element_type=F32)
 
     def phase(i, cur, nxt, opening=False):
-        base = pl.multiple_of(HEAD + i * ROWS, 32)
+        base = pl.multiple_of(HEAD + i * ROWS, ALIGN)
         for t in range(tiles):
             if opening and t + 1 < tiles:
                 dot(HEAD, t + 1, cur)
-            dot(pl.multiple_of(base + ROWS, 32), t, nxt)
+            dot(pl.multiple_of(base + ROWS, ALIGN), t, nxt)
             spans = [slice(t * BLOCK + q * 128, t * BLOCK + (q + 1) * 128) for q in range(BLOCK // 128)]
             covs = [cov_ref[:, at] for at in spans]
             softs = [soft_ref[:, at] for at in spans]
@@ -276,15 +276,15 @@
         return 0
 
     dot(HEAD, 0, y_ref)
-    acc_ref[0:HEAD, :] = jnp.zeros((HEAD, 128), F32)
     phase(jnp.int32(0), y_ref, z_ref, True)
     lax.fori_loop(0, n_blocks // 2, body, 0)
     ones = jnp.ones((16, 128), BF16)
     for s in range(ny):
         for b in range(n // 128):
-            at = pl.ds(pl.multiple_of(offs[s] + b * 128, ALIGN), 128)
+            at = pl.ds(pl.multiple_of(offs[s] + (b * 128 - HEAD), ALIGN), 128)
+            own = (infos_ref[s, 0:1, b * 128:(b + 1) * 128] > 0) & (lax.broadcasted_iota(jnp.int32, (1, 128), 1) >= HEAD - b * 128)
             got = sum(nt(ones, p)[0:1] for p in split3(acc_ref[at, :])[:2])
-            load_ref[s:s + 1, b * 128:(b + 1) * 128] = jnp.where(infos_ref[s, 0:1, b * 128:(b + 1) * 128] > 0, got, 0.0)
+            load_ref[s:s + 1, b * 128:(b + 1) * 128] = jnp.where(own, got, 0.0)
     soft = 0.0
     for r in range(nz):
         at = slice(r * cols, (r + 1) * cols)
@@ -310,8 +310,9 @@
         covs = [jnp.zeros((16, 128), F32)] * (BLOCK // 128)
         softs = [jnp.zeros((8, 128), F32)] * (BLOCK // 128)
         weights = wt_ref[pl.ds(t, 1), :]
-        for r in range(0, HEAD, 32):
-            loads = [hacc[r:r + 16, :], hacc[r + 16:r + 32, :]]
+        for r in range(0, head_ref.shape[0], 32):
+            places = [slice(k // HEAD * 128 + k % HEAD, k // HEAD * 128 + k % HEAD + 16) for k in (r, r + 16)]
+            loads = [hacc[at, :] for at in places]
             for q in range(BLOCK // 128):
                 at = slice(q * 128, (q + 1) * 128)
                 es = [jnp.exp2(hy[t, r + 16 * s:r + 16 * s + 16, at] * scale) for s in range(2)]
@@ -322,8 +323,8 @@
                 loads = [a + x for a, x in zip(loads, xs)]
                 covs[q] = covs[q] + (xs[0] + xs[1])
                 softs[q] = softs[q] + jnp.log(p[0:8] * p[8:16])
-            hacc[r:r + 16, :] = loads[0]
-            hacc[r + 16:r + 32, :] = loads[1]
+            for at, load in zip(places, loads):
+                hacc[at, :] = load
         hcov[pl.ds(t, 1), :] = jnp.concatenate([jnp.sum(v, axis=0, keepdims=True) for v in covs], axis=1)
         for q in range(BLOCK // 128):
             soft = soft + softs[q] * weights[:, q * 128:(q + 1) * 128]
@@ -358,9 +359,9 @@
     gotz[z] = (cover_ref[...] + hcov[...]) / wt_ref[...]
     ones = jnp.ones((16, 128), BF16)
     hload[...] = load_ref[...]
-    for b in range(2):
-        at = slice(b * 128, (b + 1) * 128)
-        hload[0:1, at] = load_ref[0:1, at] + sum(nt(ones, p)[0:1] for p in split3(hacc[at, :])[:2])
+    for k in range(ny):
+        part = split3(hacc[k * 128:(k + 1) * 128, :])[:2]
+        hload[k:k + 1, 0:128] = load_ref[k:k + 1, 0:128] + sum(nt(ones, p)[0:1] for p in part)
     gotc[c] = hload[...]
     pl.semaphore_wait(pltpu.get_barrier_semaphore(), len(peers))
     if last:
@@ -453,7 +454,7 @@
 
 def work_of(ny, n, cols, width):
     scr = pltpu.VMEM
-    rows = ny * n + HEAD + 3 * ROWS
+    rows = ny * n + 3 * ROWS
     total = NZ * cols
     return rows, [
         scr((rows, 2 * width), BF16),
@@ -493,7 +494,7 @@
     mu = None
     for step in range(ITERS):
         last = step == ITERS - 1
-        outs = (sd((ny, n), F32), sd((NZ, cols), F32), sd((1, 128), F32), sd((NZ, 2 * width, cols), BF16), sd((HEAD, 2 * width), BF16))
+        outs = (sd((ny, n), F32), sd((NZ, cols), F32), sd((1, 128), F32), sd((NZ, 2 * width, cols), BF16), sd((ny * HEAD, 2 * width), BF16))
         if step == 0:
             load, cover, tot, w, head, mu, coords = pl.pallas_call(
                 packed(step_kernel, step, ny),
@@ -503,10 +504,10 @@
         else:
             load, cover, tot, w, head = pl.pallas_call(
                 packed(step_kernel, step, ny),
-                out_shape=outs, in_specs=[VMEM] * 8, out_specs=(VMEM,) * 5, scratch_shapes=work,
+                out_shape=outs, in_specs=[VMEM] * 9, out_specs=(VMEM,) * 5, scratch_shapes=work,
                 compiler_params=params(), name="step",
-            )(coords, infos, turned, hq, mu, lam, wt, tot)
-        front = [scr((NZ, HEAD, cols), F32), scr((256, 128), F32), scr((NZ, cols), F32), scr((ny, n), F32)]
+            )(coords, head, infos, turned, hq, mu, lam, wt, tot)
+        front = [scr((NZ, ny * HEAD, cols), F32), scr((ny * 128, 128), F32), scr((NZ, cols), F32), scr((ny, n), F32)]
         scratch = [scr((NZ, NZ, cols), F32), scr((nc, ny, n), F32), scr((ny, ny, n), F32), scr((ny, n), F32),
                    dma((NZ - 1,)), dma((NZ - 1,)), dma((nc - 1,)), dma((nc - 1,)), dma((ny - 1,)), dma((ny - 1,))]
         if not last:

time: 85.3 us -> 83 us (0.973)
  Pallas kernels: 84.4 us -> 82.1 us
    pallas_call x2, Pallas kernels: 15.4 us -> 13.5 us  [local(): pl.pallas_call(packed(step_kernel, step, ny), out_shape=outs, in_specs=[V...]
    pallas_call x1, Pallas kernels: 7.74 us -> 6.75 us  [local(): pl.pallas_call(packed(step_kernel, step, ny), out_shape=outs + (sd((ny, n...]
where the time goes in v6:
time: 83 us; the launch traced here: 82.9 us
  Pallas kernels  82.1 us (99%)
    pallas_call x2, Pallas kernels, local(): pl.pallas_call(packed(reduce_kernel, step, ny, nc), out_shape=(sd((NZ, co...  23.8 us
    pallas_call x1, Pallas kernels, local(): pl.pallas_call(functools.partial(gather_kernel, ny), out_shape=(sd((ny, n...  21.9 us
    pallas_call x1, Pallas kernels, local(): pl.pallas_call(packed(reduce_kernel, step, ny, nc), out_shape=(sd((nf, 1,...  15 us
    pallas_call x2, Pallas kernels, local(): pl.pallas_call(packed(step_kernel, step, ny), out_shape=outs, in_specs=[V...  13.5 us
    pallas_call x1, Pallas kernels, local(): pl.pallas_call(packed(step_kernel, step, ny), out_shape=outs + (sd((ny, n...  6.75 us

profile of v6, /device:TPU:1, one launch (start us, length us, event | category | flops | bytes accessed | tf_op | source)
XLA Modules:
  0.0 82.9 jit_solution(17007181643561866051)
XLA Ops:
  0.6 21.9 %gather.1 = (bf16[4,512,128]{2,1,0:T(8,128)(2,1)S(1)}, f32[4,8,512]{2,1,0:T(8,128)S(1)}, f32[8,512]{1,0:T(8,128)S(1)}, f32[8,512]{1,0:T(8,128)S(1)}, f32[1,128]{...) custom-call(bf16[512,128]{1,0:T(8,128)(2,1)} %cust_hbm.1, ...), custom_call_target="tpu_custom_call" | custom-call | tf_op jit(solution)/shard_map/gather/pallas_call | solution.py:479
  22.5 6.8 %step.3 = (f32[4,512]{1,0:T(4,128)S(1)}, f32[8,512]{1,0:T(8,128)S(1)}, f32[1,128]{1,0:T(1,128)S(1)}, bf16[8,256,512]{2,1,0:T(8,128)(2,1)S(1)}, bf16[320,256]{1,0...) custom-call(bf16[4,512,128]{2,1,0:T(8,128)(2,1)S(1)} %get-tuple-element.41.refs_0_, ...), custom_call_target="tpu_custom_call" | custom-call | tf_op jit(solution)/shard_map/step/pallas_call | solution.py:499
  29.3 13.8 %reduce.3 = (f32[8,512]{1,0:T(8,128)S(1)}, f32[4,512]{1,0:T(4,128)S(1)}, f32[1,128]{1,0:T(1,128)S(1)}) custom-call(f32[4,512]{1,0:T(4,128)S(1)} %get-tuple-element.50.refs_0_, f32[8,512]{1,0:T(8,128)S(1)} %get-tuple-element.51.refs_1_, f32[8,512]{1,0:T(8,128)S(1)} %get-tuple-element.45.refs_4_.refs_2_, ...), custom_call_target="tpu_custom_call" | custom-call | tf_op jit(solution)/shard_map/reduce/pallas_call | solution.py:514
  43.1 6.8 %step.4 = (f32[4,512]{1,0:T(4,128)S(1)}, f32[8,512]{1,0:T(8,128)S(1)}, f32[1,128]{1,0:T(1,128)S(1)}, bf16[8,256,512]{2,1,0:T(8,128)(2,1)S(1)}, bf16[320,256]{1,0:T(8,128)(2,1)S(1)}) custom-call(bf16[2528,128]{1,0:T(8,128)(2,1)S(1)} %get-tuple-element.48.refs_0_, bf16[320,256]{1,0:T(8,128)(2,1)S(1)} %get-tuple-element.49.refs_8_.refs_1_, ...), custom_call_target="tpu_custom_call" | custom-call | tf_op jit(solution)/shard_map/step/pallas_call | solution.py:505
  49.9 10.1 %reduce.4 = (f32[8,512]{1,0:T(8,128)S(1)}, f32[4,512]{1,0:T(4,128)S(1)}, f32[1,128]{1,0:T(1,128)S(1)}) custom-call(f32[4,512]{1,0:T(4,128)S(1)} %get-tuple-element.59.refs_0_, f32[8,512]{1,0:T(8,128)S(1)} %get-tuple-element.60.refs_1_, f32[8,512]{1,0:T(8,128)S(1)} %get-tuple-element.56.refs_6_.refs_2_, ...), custom_call_target="tpu_custom_call" | custom-call | tf_op jit(solution)/shard_map/reduce/pallas_call | solution.py:514
  59.9 6.7 %step.5 = (f32[4,512]{1,0:T(4,128)S(1)}, f32[8,512]{1,0:T(8,128)S(1)}, f32[1,128]{1,0:T(1,128)S(1)}, bf16[8,256,512]{2,1,0:T(8,128)(2,1)S(1)}, bf16[320,256]{1,0:T(8,128)(2,1)S(1)}) custom-call(bf16[2528,128]{1,0:T(8,128)(2,1)S(1)} %get-tuple-element.48.refs_0_, bf16[320,256]{1,0:T(8,128)(2,1)S(1)} %get-tuple-element.58.refs_8_.refs_1_, ...), custom_call_target="tpu_custom_call" | custom-call | tf_op jit(solution)/shard_map/step/pallas_call | solution.py:505
  66.6 15.0 %reduce.5 = (f32[32,1,512]{2,1,0:T(1,128)S(1)}, f32[1,512]{1,0:T(1,128)S(1)}, f32[1,128]{1,0:T(1,128)S(1)}) custom-call(f32[4,512]{1,0:T(4,128)S(1)} %get-tuple-element.66.refs_0_, f32[8,512]{1,0:T(8,128)S(1)} %get-tuple-element.67.refs_1_, f32[8,512]{1,0:T(8,128)S(1)} %get-tuple-element.64.refs_6_.refs_2_, ...), custom_call_target="tpu_custom_call" | custom-call | tf_op jit(solution)/shard_map/reduce/pallas_call | solution.py:521
  81.6 1.2 %finish.1 = (f32[32,1,512]{2,1,0:T(1,128)}, f32[1,512]{1,0:T(1,128)}, f32[3]{0:T(128)}) custom-call(f32[32,1,512]{2,1,0:T(1,128)S(1)} %get-tuple-element.73.lam_ref, f32[1,512]{1,0:T(1,128)S(1)} %get-tuple-element.74.cap_ref, f32[1,128]{1,0:T(1,128)S(1)} %get-tuple-element.75.bound_ref), custom_call_target="tpu_custom_call" | custom-call | tf_op jit(solution)/shard_map/finish/pallas_call | solution.py:529

commit v7 on v6

--- a/solution.py
+++ b/solution.py
@@ -15,7 +15,7 @@
 ROWS = 160
 HEAD = 80
 BLOCK = 512
-CHUNKS = 8
+CHUNKS = 16
 NZ = 8
 F32 = jnp.float32
 BF16 = jnp.bfloat16

time: 83 us -> 84.2 us (1.014)
  Pallas kernels: 82.1 us -> 83.3 us
    pallas_call x1, Pallas kernels: 21.9 us -> 22.7 us  [local(): pl.pallas_call(functools.partial(gather_kernel, ny), out_shape=(sd((ny, n...]
where the time goes in v7:
time: 84.2 us; the launch traced here: 84.1 us
  Pallas kernels  83.3 us (99%)
    pallas_call x2, Pallas kernels, local(): pl.pallas_call(packed(reduce_kernel, step, ny, nc), out_shape=(sd((NZ, co...  24.1 us
    pallas_call x1, Pallas kernels, local(): pl.pallas_call(functools.partial(gather_kernel, ny), out_shape=(sd((ny, n...  22.7 us
    pallas_call x1, Pallas kernels, local(): pl.pallas_call(packed(reduce_kernel, step, ny, nc), out_shape=(sd((nf, 1,...  15 us
    pallas_call x2, Pallas kernels, local(): pl.pallas_call(packed(step_kernel, step, ny), out_shape=outs, in_specs=[V...  13.5 us
    pallas_call x1, Pallas kernels, local(): pl.pallas_call(packed(step_kernel, step, ny), out_shape=outs + (sd((ny, n...  6.76 us

profile of v7, /device:TPU:1, one launch (start us, length us, event | category | flops | bytes accessed | tf_op | source)
XLA Modules:
  0.0 84.1 jit_solution(6409670355115430732)
XLA Ops:
  0.6 22.7 %gather.1 = (bf16[4,512,128]{2,1,0:T(8,128)(2,1)S(1)}, f32[4,8,512]{2,1,0:T(8,128)S(1)}, f32[8,512]{1,0:T(8,128)S(1)}, f32[8,512]{1,0:T(8,128)S(1)}, f32[1,128]{...) custom-call(bf16[512,128]{1,0:T(8,128)(2,1)} %cust_hbm.1, ...), custom_call_target="tpu_custom_call" | custom-call | tf_op jit(solution)/shard_map/gather/pallas_call | solution.py:479
  23.4 6.8 %step.3 = (f32[4,512]{1,0:T(4,128)S(1)}, f32[8,512]{1,0:T(8,128)S(1)}, f32[1,128]{1,0:T(1,128)S(1)}, bf16[8,256,512]{2,1,0:T(8,128)(2,1)S(1)}, bf16[320,256]{1,0...) custom-call(bf16[4,512,128]{2,1,0:T(8,128)(2,1)S(1)} %get-tuple-element.41.refs_0_, ...), custom_call_target="tpu_custom_call" | custom-call | tf_op jit(solution)/shard_map/step/pallas_call | solution.py:499
  30.1 14.1 %reduce.3 = (f32[8,512]{1,0:T(8,128)S(1)}, f32[4,512]{1,0:T(4,128)S(1)}, f32[1,128]{1,0:T(1,128)S(1)}) custom-call(f32[4,512]{1,0:T(4,128)S(1)} %get-tuple-element.50.refs_0_, f32[8,512]{1,0:T(8,128)S(1)} %get-tuple-element.51.refs_1_, f32[8,512]{1,0:T(8,128)S(1)} %get-tuple-element.45.refs_4_.refs_2_, ...), custom_call_target="tpu_custom_call" | custom-call | tf_op jit(solution)/shard_map/reduce/pallas_call | solution.py:514
  44.3 6.8 %step.4 = (f32[4,512]{1,0:T(4,128)S(1)}, f32[8,512]{1,0:T(8,128)S(1)}, f32[1,128]{1,0:T(1,128)S(1)}, bf16[8,256,512]{2,1,0:T(8,128)(2,1)S(1)}, bf16[320,256]{1,0:T(8,128)(2,1)S(1)}) custom-call(bf16[2528,128]{1,0:T(8,128)(2,1)S(1)} %get-tuple-element.48.refs_0_, bf16[320,256]{1,0:T(8,128)(2,1)S(1)} %get-tuple-element.49.refs_8_.refs_1_, ...), custom_call_target="tpu_custom_call" | custom-call | tf_op jit(solution)/shard_map/step/pallas_call | solution.py:505
  51.1 10.0 %reduce.4 = (f32[8,512]{1,0:T(8,128)S(1)}, f32[4,512]{1,0:T(4,128)S(1)}, f32[1,128]{1,0:T(1,128)S(1)}) custom-call(f32[4,512]{1,0:T(4,128)S(1)} %get-tuple-element.59.refs_0_, f32[8,512]{1,0:T(8,128)S(1)} %get-tuple-element.60.refs_1_, f32[8,512]{1,0:T(8,128)S(1)} %get-tuple-element.56.refs_6_.refs_2_, ...), custom_call_target="tpu_custom_call" | custom-call | tf_op jit(solution)/shard_map/reduce/pallas_call | solution.py:514
  61.1 6.7 %step.5 = (f32[4,512]{1,0:T(4,128)S(1)}, f32[8,512]{1,0:T(8,128)S(1)}, f32[1,128]{1,0:T(1,128)S(1)}, bf16[8,256,512]{2,1,0:T(8,128)(2,1)S(1)}, bf16[320,256]{1,0:T(8,128)(2,1)S(1)}) custom-call(bf16[2528,128]{1,0:T(8,128)(2,1)S(1)} %get-tuple-element.48.refs_0_, bf16[320,256]{1,0:T(8,128)(2,1)S(1)} %get-tuple-element.58.refs_8_.refs_1_, ...), custom_call_target="tpu_custom_call" | custom-call | tf_op jit(solution)/shard_map/step/pallas_call | solution.py:505
  67.8 15.0 %reduce.5 = (f32[32,1,512]{2,1,0:T(1,128)S(1)}, f32[1,512]{1,0:T(1,128)S(1)}, f32[1,128]{1,0:T(1,128)S(1)}) custom-call(f32[4,512]{1,0:T(4,128)S(1)} %get-tuple-element.66.refs_0_, f32[8,512]{1,0:T(8,128)S(1)} %get-tuple-element.67.refs_1_, f32[8,512]{1,0:T(8,128)S(1)} %get-tuple-element.64.refs_6_.refs_2_, ...), custom_call_target="tpu_custom_call" | custom-call | tf_op jit(solution)/shard_map/reduce/pallas_call | solution.py:521
  82.8 1.2 %finish.1 = (f32[32,1,512]{2,1,0:T(1,128)}, f32[1,512]{1,0:T(1,128)}, f32[3]{0:T(128)}) custom-call(f32[32,1,512]{2,1,0:T(1,128)S(1)} %get-tuple-element.73.lam_ref, f32[1,512]{1,0:T(1,128)S(1)} %get-tuple-element.74.cap_ref, f32[1,128]{1,0:T(1,128)S(1)} %get-tuple-element.75.bound_ref), custom_call_target="tpu_custom_call" | custom-call | tf_op jit(solution)/shard_map/finish/pallas_call | solution.py:529
